TPU v7x, 32 devices: a whole 2x2x4 slice. The times are simulated.
32 devices in a mesh: rep: 1, dp: 32 (over x, y, z, core).
Axes of the slice: x: 2, y: 2, z: 4, core: 2. Of those that a mesh axis runs over, the one named last changes fastest.
Arguments:
- x: bfloat16 [32, 2048, 640], P(('rep', 'dp'))
- dy: bfloat16 [32, 2048, 640], P(('rep', 'dp'))
- w_gate: bfloat16 [2, 640, 2560], replicated
- w_up: bfloat16 [2, 640, 2560], replicated
- w_down: bfloat16 [2, 2560, 640], replicated
- m_w_gate: float32 [2, 640, 2560], P(None, 'dp')
- m_w_up: float32 [2, 640, 2560], P(None, 'dp')
- m_w_down: float32 [2, 2560, 640], P(None, 'dp')
- v_w_gate: float32 [2, 640, 2560], P(None, 'dp')
- v_w_up: float32 [2, 640, 2560], P(None, 'dp')
- v_w_down: float32 [2, 2560, 640], P(None, 'dp')
Outputs:
- output 1: bfloat16 [2, 640, 2560], P('rep')
- output 2: bfloat16 [2, 640, 2560], P('rep')
- output 3: bfloat16 [2, 2560, 640], P('rep')
- output 4: float32 [2, 640, 2560], P('rep', 'dp')
- output 5: float32 [2, 640, 2560], P('rep', 'dp')
- output 6: float32 [2, 2560, 640], P('rep', 'dp')
- output 7: float32 [2, 640, 2560], P('rep', 'dp')
- output 8: float32 [2, 640, 2560], P('rep', 'dp')
- output 9: float32 [2, 2560, 640], P('rep', 'dp')
All inputs are finite; a program needn't handle non-finite values.
Results may differ from a plain program's by a relative error of at most 0.022.
Values are sent between devices in bfloat16 or wider.
A program may use at most 2 GiB of HBM per device.

v0:
```python
import jax
import jax.numpy as jnp
from jax import lax

NAMES = ("w_gate", "w_up", "w_down")


def matmul(a, w):
    return jnp.dot(a, w, preferred_element_type=jnp.float32).astype(jnp.bfloat16)


def normed(h):
    wide = h.astype(jnp.float32)
    scale = lax.rsqrt(jnp.mean(wide**2, -1, keepdims=True) + 1e-6)
    return (wide * scale).astype(jnp.bfloat16)


def layer(h, w):
    a = normed(h)
    gate = jnp.dot(a, w["w_gate"], preferred_element_type=jnp.float32)
    up = jnp.dot(a, w["w_up"], preferred_element_type=jnp.float32)
    return h + matmul((jax.nn.silu(gate) * up).astype(jnp.bfloat16), w["w_down"])


def adamw(w, m, v, g):
    m = 0.9 * m + 0.1 * g
    v = 0.95 * v + 0.05 * g * g
    step = m * lax.rsqrt(v + 1e-8) + 0.1 * w
    return (w - 0.02 * step).astype(jnp.bfloat16), m, v


def clipped(gradients, sum_of_squares, count):
    factor = jnp.minimum(1.0, 0.5 * lax.rsqrt(sum_of_squares / count + 1e-30))
    return [g * factor for g in gradients]


def stack(weights, h):
    for number in range(weights["w_gate"].shape[0]):
        h = layer(h, {name: w[number] for name, w in weights.items()})
    return h


def solution(mesh):
    groups = mesh.shape["rep"]

    def step(x, dy, *arrays):
        weights, m, v = (arrays[i : i + 3] for i in (0, 3, 6))
        x, dy = (t.reshape(groups, -1, *t.shape[1:]) for t in (x, dy))

        def of_a_group(x, dy):
            _, back = jax.vjp(lambda w: stack(w, x), dict(zip(NAMES, weights, strict=True)))
            by_weights = back(dy)[0]
            gradients = [by_weights[name].astype(jnp.float32) for name in NAMES]
            gradients = clipped(gradients, sum(jnp.sum(g * g) for g in gradients), sum(g.size for g in gradients))
            new = [adamw(w.astype(jnp.float32), m, v, g) for w, m, v, g in zip(weights, m, v, gradients, strict=True)]
            return tuple(one[which] for which in range(3) for one in new)

        return tuple(t.reshape(-1, *t.shape[2:]) for t in jax.vmap(of_a_group)(x, dy))

    return step
```

profile of v0, /device:TPU:0, one launch (start us, length us, event | category | flops | bytes accessed | tf_op | source)
XLA Modules:
  0.0 1810.6 jit_solution(18008899455319665702)
XLA Ops:
  14.1 14.3 fusion.173
  28.4 21.8 %fusion.150 = (bf16[1,2048,2560]{2,1,0:T(8,128)(2,1)}, f32[2048,2560]{1,0:T(8,128)}) fusion(f32[2048,2560]{1,0:T(8,128)} %fusion.173, bf16[2,640,2560]{2,1,0:T(8,128)(2,1)} %param.17, bf16[1,2048,640]{1,2,0:T(8,128)(2,1)S(1)} %fusion.157), kind=kOutput, calls=%fused_computation.189 | convolution fusion | flops 6742343680 | bytes 58327040 | tf_op jit(solution)/vmap(jvp())/dot_general | solution.py:21
  50.3 11.6 fusion.160
  63.2 15.0 fusion.166
  78.3 10.6 convolution_convert_fusion.1
  88.9 30.9 %fusion.139 = (bf16[1,2048,2560]{2,1,0:T(8,128)(2,1)}, bf16[1,2048,2560]{2,1,0:T(8,128)(2,1)}, f32[2048,2560]{1,0:T(8,128)}) fusion(f32[2048,2560]{1,0:T(8,128)} %fusion.166, bf16[2048,2560]{1,0:T(8,128)(2,1)} %convolution_convert_fusion.1, bf16[2,640,2560]{2,1,0:T(8,128)(2,1)S(1)} %bitcast.643, bf16[1,2048,640]{1,2,0:T(8,128)(2,1)S(1)} %fusion.161), kind=kOutput, calls=%fused_computation.173 | convolution fusion | flops 6789529600 | bytes 79298560 | tf_op jit(solution)/vmap(jvp())/dot_general | solution.py:20
  119.8 19.3 %fusion.149 = bf16[1,2048,2560]{2,1,0:T(8,128)(2,1)} fusion(f32[2048,2560]{1,0:T(8,128)} %fusion.166, f32[2048,2560]{1,0:T(8,128)} %get-tuple-element.305), kind=kLoop, calls=%fused_computation.187 | loop fusion | flops 31457280 | bytes 52428800 | tf_op jit(solution)/vmap(jvp())/convert_element_type | solution.py:22
  139.1 14.6 copy.26
  153.7 177.9 %while.16 = (bf16[1,2048,2560]{1,2,0:T(8,128)(2,1)}, bf16[1,2048,640]{2,1,0:T(8,128)(2,1)S(1)}, f32[80,640]{1,0:T(8,128)S(1)}, f32[80,640]{1,0:T(8,128)}, u32[]{...) while((bf16[1,2048,2560]{1,2,0:T(8,128)(2,1)}, ...), condition=%wide.windowed_dot_general_cond_rs.4.clone, body=%wide.windowed_dot_general_body_rs.4.clone.sunk | while | flops 841789440 | bytes 75530856 | solution.py:9
  154.4 6.0 collective-permute-start.17
  334.4 14.7 copy.28
  349.1 10.8 fusion.184
  360.0 9.1 fusion.162
  374.2 178.7 %while.17 = (bf16[1,2048,640]{2,1,0:T(8,128)(2,1)}, bf16[1,2048,2560]{1,2,0:T(8,128)(2,1)}, f32[640,80]{0,1:T(8,128)S(1)}, f32[640,80]{0,1:T(8,128)}, u32[]{:T(1...) while((bf16[1,2048,640]{2,1,0:T(8,128)(2,1)}, ...), condition=%wide.windowed_dot_general_cond_rs.5.clone, body=%wide.windowed_dot_general_body_rs.5.clone.sunk | while | flops 841789440 | bytes 75530856 | solution.py:9
  553.6 231.2 %while.14 = (bf16[1,2048,2560]{2,1,0:T(8,128)(2,1)}, bf16[1,2048,640]{1,2,0:T(8,128)(2,1)S(1)}, f32[2560,20]{0,1:T(8,128)S(1)}, f32[2560,20]{0,1:T(8,128)}, u32[...) while((bf16[1,2048,2560]{2,1,0:T(8,128)(2,1)}, ...), condition=%wide.windowed_dot_general_cond_rs.2.clone, body=%wide.windowed_dot_general_body_rs.2.clone.sunk | while | flops 839823360 | bytes 34407020 | solution.py:21
  573.5 5.8 fusion.331
  589.7 5.8 fusion.329
  618.7 5.8 fusion.329
  631.6 5.8 fusion.331
  647.7 5.8 fusion.329
  676.6 5.8 fusion.329
  785.5 29.2 %convert_multiply_fusion = (bf16[1,2048,2560]{2,1,0:T(8,128)(2,1)}, bf16[1,2048,2560]{2,1,0:T(8,128)(2,1)}) fusion(f32[2048,2560]{1,0:T(8,128)} %fusion.173, f32[2048,2560]{1,0:T(8,128)} %get-tuple-element.302, bf16[2,2560,640]{2,1,0:T(8,128)(2,1)} %param.15, bf16[1,2048,640]{1,2,0:T(8,128)(2,1)} %copy-done.8), kind=kOutput, calls=%fused_computation.168 | convolution fusion | flops 6794772480 | bytes 68812800 | tf_op jit(solution)/vmap(transpose(jvp()))/dot_general | solution.py:9
  814.7 233.5 %while.15 = (bf16[1,2048,2560]{2,1,0:T(8,128)(2,1)}, bf16[1,2048,640]{1,2,0:T(8,128)(2,1)S(1)}, f32[2560,20]{0,1:T(8,128)}, f32[2560,20]{0,1:T(8,128)}, u32[]{:T...) while((bf16[1,2048,2560]{2,1,0:T(8,128)(2,1)}, ...), condition=%wide.windowed_dot_general_cond_rs.3.clone, body=%wide.windowed_dot_general_body_rs.3.clone.sunk | while | flops 839823360 | bytes 33587792 | solution.py:21
  1048.2 236.4 %while.12 = (bf16[1,2048,2560]{2,1,0:T(8,128)(2,1)}, bf16[1,2048,640]{1,2,0:T(8,128)(2,1)}, f32[2560,20]{0,1:T(8,128)}, f32[2560,20]{0,1:T(8,128)}, u32[]{:T(128...) while((bf16[1,2048,2560]{2,1,0:T(8,128)(2,1)}, ...), condition=%wide.windowed_dot_general_cond_rs.clone, body=%wide.windowed_dot_general_body_rs.clone.sunk | while | flops 839823360 | bytes 33587792 | solution.py:20
  1055.0 6.0 fusion.313
  1068.3 6.0 fusion.315
  1084.8 6.0 fusion.313
  1098.0 6.0 fusion.315
  1114.6 6.0 fusion.313
  1127.8 6.0 fusion.315
  1144.4 6.0 fusion.313
  1157.6 6.0 fusion.315
  1174.2 6.0 fusion.313
  1187.4 6.0 fusion.315
  1203.9 6.0 fusion.313
  1217.2 6.0 fusion.315
  1233.7 6.0 fusion.313
  1247.0 6.0 fusion.315
  1263.5 6.0 fusion.313
  1276.7 6.0 fusion.315
  1284.6 231.1 %while.13 = (bf16[1,2048,2560]{2,1,0:T(8,128)(2,1)}, bf16[1,2048,640]{1,2,0:T(8,128)(2,1)S(1)}, f32[2560,20]{0,1:T(8,128)S(1)}, f32[2560,20]{0,1:T(8,128)}, u32[...) while((bf16[1,2048,2560]{2,1,0:T(8,128)(2,1)}, ...), condition=%wide.windowed_dot_general_cond_rs.1.clone, body=%wide.windowed_dot_general_body_rs.1.clone.sunk | while | flops 839823360 | bytes 34407020 | solution.py:20
  1517.1 7.9 collective-permute-done.27
  1534.9 38.4 %all-reduce.10 = f32[]{:T(128)} all-reduce(f32[]{:T(128)S(6)} %add.180), channel_id=13, replica_groups=mesh['rep'=1,'dp'=32] {'dp'}, use_global_device_ids=true, to_apply=%region_3.4.clone | all-reduce | flops 1 | bytes 8 | tf_op jit(solution)/vmap()/reduce_sum | solution.py:54
  1585.3 63.3 %all-gather.14.cloned.1.call-done = bf16[1,2,2560,640]{3,2,1,0:T(8,128)(2,1)} async-done(((bf16[1,2,80,640]{3,2,1,0:T(8,128)(2,1)}), bf16[1,2,2560,640]{3,2,1,0:T(8,128)(2,1)}) %all-gather.14.cloned.1.call-update) | async-done | bytes 6553616 | tf_op jit(solution)/reshape | solution.py:58
  1648.6 72.9 %all-gather.12.cloned.1.call-done = bf16[1,2,640,2560]{3,1,0,2:T(2,128)(2,1)} async-done(((bf16[1,2,20,2560]{3,1,0,2:T(2,128)(2,1)}), bf16[1,2,640,2560]{3,1,0,2:T(2,128)(2,1)}) %all-gather.12.cloned.1.call-update) | async-done | bytes 6553616 | tf_op jit(solution)/reshape | solution.py:58
  1721.4 6.7 copy.70
  1728.1 65.9 %all-gather.10.cloned.1.call-done = bf16[1,2,640,2560]{3,1,0,2:T(2,128)(2,1)} async-done(((bf16[1,2,20,2560]{3,1,0,2:T(2,128)(2,1)}), bf16[1,2,640,2560]{3,1,0,2:T(2,128)(2,1)}) %all-gather.10.cloned.1.call-update) | async-done | bytes 6553616 | tf_op jit(solution)/reshape | solution.py:58
  1794.0 6.8 copy.71
  (833 shorter events, 1190.3 us)
Async XLA Ops:
  7.2 1641.4 %all-gather.14.cloned.1.call-start = ((), (), s32[]{:S(2)}) async-start(), calls=%async_computation.2 | async-start | bytes 6758400 | tf_op jit(solution)/reshape | solution.py:58
  331.6 1197.0 %collective-permute-start.28 = (f32[80,640]{1,0:T(8,128)}, f32[80,640]{1,0:T(8,128)}, u32[]{:S(2)}, u32[]{:S(2)}) collective-permute-start(f32[80,640]{1,0:T(8,128)} %get-tuple-element.45), channel_id=32, source_target_pairs={{0,1},{1,2},{2,3},{3,4},{4,5},{5,6},{6,7},{7,8},{8,9},{9,10},{10,1... | collective-permute-start | bytes 614408 | tf_op jit(solution)/vmap(transpose(jvp()))/dot_general | solution.py:9
  552.9 976.7 %collective-permute-start.29 = (f32[640,80]{0,1:T(8,128)}, f32[640,80]{0,1:T(8,128)}, u32[]{:S(2)}, u32[]{:S(2)}) collective-permute-start(f32[640,80]{0,1:T(8,128)} %get-tuple-element.47), channel_id=38, source_target_pairs={{0,1},{1,2},{2,3},{3,4},{4,5},{5,6},{6,7},{7,8},{8,9},{9,10},{10,1... | collective-permute-start | bytes 614408 | tf_op jit(solution)/vmap(transpose(jvp()))/dot_general | solution.py:9
  554.3 12.1 collective-permute-start.8
  568.2 12.0 collective-permute-start.11
  583.7 11.9 collective-permute-start.8
  597.3 11.8 collective-permute-start.11
  612.6 11.9 collective-permute-start.8
  626.3 11.8 collective-permute-start.11
  641.6 11.9 collective-permute-start.8
  670.6 11.9 collective-permute-start.8
  684.2 11.8 collective-permute-start.11
  699.5 11.9 collective-permute-start.8
  728.5 11.9 collective-permute-start.8
  742.2 11.8 collective-permute-start.11
  757.5 11.9 collective-permute-start.8
  784.8 731.0 %collective-permute-start.26 = (f32[2560,20]{0,1:T(8,128)}, f32[2560,20]{0,1:T(8,128)}, u32[]{:S(2)}, u32[]{:S(2)}) collective-permute-start(f32[2560,20]{0,1:T(8,128)} %get-tuple-element.41), channel_id=19, source_target_pairs={{0,1},{1,2},{2,3},{3,4},{4,5},{5,6},{6,7},{7,8},{8,9},{9,10},{10,1... | collective-permute-start | bytes 614408 | tf_op jit(solution)/vmap(transpose(jvp()))/dot_general | solution.py:21
  815.4 11.9 collective-permute-start.12
  843.9 12.8 collective-permute-start.12
  873.3 12.8 collective-permute-start.12
  902.8 12.8 collective-permute-start.12
  932.2 12.8 collective-permute-start.12
  961.6 12.8 collective-permute-start.12
  991.0 12.8 collective-permute-start.12
  1020.5 12.8 collective-permute-start.12
  1049.0 12.1 collective-permute-start
  1077.8 13.0 collective-permute-start
  1107.6 13.0 collective-permute-start
  1137.4 13.0 collective-permute-start
  1167.2 13.0 collective-permute-start
  1196.9 13.0 collective-permute-start
  1226.7 13.0 collective-permute-start
  1256.5 13.0 collective-permute-start
  1285.6 11.9 collective-permute-start.4
  1299.2 11.8 collective-permute-start.7
  1314.6 11.9 collective-permute-start.4
  1343.5 11.9 collective-permute-start.4
  1357.2 11.8 collective-permute-start.7
  1372.5 11.9 collective-permute-start.4
  1401.5 11.9 collective-permute-start.4
  1415.1 11.8 collective-permute-start.7
  1430.5 11.9 collective-permute-start.4
  1459.4 11.9 collective-permute-start.4
  1473.1 11.8 collective-permute-start.7
  1488.4 11.9 collective-permute-start.4
  1515.9 16.3 collective-permute-start.25
  1576.3 145.1 %all-gather.12.cloned.1.call-start = ((), (), s32[]{:S(2)}) async-start(), calls=%async_computation.1 | async-start | bytes 6758400 | tf_op jit(solution)/reshape | solution.py:58
  1578.6 215.4 %all-gather.10.cloned.1.call-start = ((), (), s32[]{:S(2)}) async-start(), calls=%async_computation | async-start | bytes 6758400 | tf_op jit(solution)/reshape | solution.py:58
  (214 other events, 2514.6 us)
Sparse Core Ops, SparseCore 0:
  1576.5 72.0 all-gather.13
  1652.0 69.3 all-gather.11
  1724.9 69.0 all-gather.9
where the time goes:
time: 1820 us; the launch traced here: 1810 us
  matrix products  589 us (32%)
  starting transfers between devices  517 us (28%)
  waiting for transfers between devices  305 us (17%)
  other arithmetic  267 us (15%)
  local copies, waits for them, and re-layouts  74.3 us (4%)
  blocking collectives  38.4 us (2%)
    dot_general x35, matrix products, layer(): gate = jnp.dot(a, w['w_gate'], preferred_element_type=jnp.float32)  242 us
    dot_general x35, matrix products, layer(): up = jnp.dot(a, w['w_up'], preferred_element_type=jnp.float32)  233 us
    reshape x3, waiting for transfers between devices, step(): t.reshape(-1, *t.shape[2:])  202 us
    dot_general x66, starting transfers between devices, matmul(): jnp.dot(a, w, preferred_element_type=jnp.float32).astype(jnp.bfloat16)  174 us
    dot_general x66, starting transfers between devices, layer(): up = jnp.dot(a, w['w_up'], preferred_element_type=jnp.float32)  171 us
    dot_general x66, starting transfers between devices, layer(): gate = jnp.dot(a, w['w_gate'], preferred_element_type=jnp.float32)  171 us
    dot_general x35, matrix products, matmul(): jnp.dot(a, w, preferred_element_type=jnp.float32).astype(jnp.bfloat16)  113 us
    dot_general x96, other arithmetic  98.7 us
  transfers between devices with their start and end apart: 201, of which 39 were waited for; matrix products, arithmetic and copies ran while one was open for 41% of the time, Pallas kernels for 0%

commit v1 on v0

v1 whole, which is shorter than its diff:
```python
import jax
import jax.numpy as jnp
from jax import lax
from jax.sharding import PartitionSpec as P

F32, BF16 = jnp.float32, jnp.bfloat16
COUNT = 6 * 640 * 2560


def dot(a, b, ca, cb):
    return lax.dot_general(a, b, (((ca,), (cb,)), ((), ())), preferred_element_type=F32)


def norm_scale(h):
    wide = h.astype(F32)
    return wide, lax.rsqrt(jnp.mean(wide**2, -1, keepdims=True) + 1e-6)


def hidden(a, wg, wu):
    gate, up = dot(a, wg, 1, 0), dot(a, wu, 1, 0)
    return gate, up, (jax.nn.silu(gate) * up).astype(BF16)


def hidden_back(ds, gate, up):
    ds = ds.astype(F32)
    sig = jax.nn.sigmoid(gate)
    d_up = (ds * (gate * sig)).astype(BF16)
    d_gate = (ds * up * (sig * (1 + gate * (1 - sig)))).astype(BF16)
    return d_gate, d_up


def gradients(x, dy, wg, wu, wd):
    wide0, r0 = norm_scale(x)
    a1 = (wide0 * r0).astype(BF16)
    gate1, up1, s1 = hidden(a1, wg[0], wu[0])
    h1 = x + dot(s1, wd[0], 1, 0).astype(BF16)
    wide1, r1 = norm_scale(h1)
    a2 = (wide1 * r1).astype(BF16)
    gate2, up2, s2 = hidden(a2, wg[1], wu[1])

    ds2 = dot(dy, wd[1], 1, 1).astype(BF16)
    d_gate2, d_up2 = hidden_back(ds2, gate2, up2)
    da2 = (dot(d_gate2, wg[1], 1, 1).astype(BF16) + dot(d_up2, wu[1], 1, 1).astype(BF16)).astype(F32)
    back = da2 * r1 - wide1 * (r1**3 * jnp.mean(da2 * wide1, -1, keepdims=True))
    dh1 = dy + back.astype(BF16)
    ds1 = dot(dh1, wd[0], 1, 1).astype(BF16)
    d_gate1, d_up1 = hidden_back(ds1, gate1, up1)

    terms = ((a1, d_gate1), (a1, d_up1), (s1, dh1)), ((a2, d_gate2), (a2, d_up2), (s2, dy))
    return [[dot(a, b, 0, 0).astype(BF16) for a, b in layer] for layer in terms]


def adamw(w, m, v, g):
    m = 0.9 * m + 0.1 * g
    v = 0.95 * v + 0.05 * g * g
    step = m * lax.rsqrt(v + 1e-8) + 0.1 * w
    return (w - 0.02 * step).astype(BF16), m, v


def solution(mesh):
    n = mesh.shape["dp"]

    def body(x, dy, *arrays):
        w, m, v = (arrays[i : i + 3] for i in (0, 3, 6))
        me = lax.axis_index("dp")
        terms = gradients(x[0], dy[0], *w)
        summed = [[None] * 3 for _ in range(2)]
        for layer in (1, 0):
            for which in (2, 0, 1):
                term = terms[layer][which]
                rows, columns = term.shape
                flat = lax.psum_scatter(term.reshape(n * 400, 128), "dp", scatter_dimension=0, tiled=True)
                summed[layer][which] = flat.reshape(rows // n, columns)
        g = [jnp.stack([summed[layer][which] for layer in range(2)]).astype(F32) for which in range(3)]
        total = lax.psum(sum(jnp.sum(t * t) for t in g), "dp")
        factor = jnp.minimum(1.0, 0.5 * lax.rsqrt(total / COUNT + 1e-30))
        new = []
        for which in range(3):
            rows = w[which].shape[1] // n
            mine = lax.dynamic_slice_in_dim(w[which], me * rows, rows, 1).astype(F32)
            new.append(adamw(mine, m[which], v[which], g[which] * factor))
        weights = [lax.all_gather(one[0], "dp", axis=1, tiled=True) for one in new]
        return (*weights, *(one[1] for one in new), *(one[2] for one in new))

    moments = P(None, "dp", None)
    return jax.shard_map(
        body,
        mesh=mesh,
        in_specs=(P(("rep", "dp")), P(("rep", "dp")), *[P()] * 3, *[moments] * 6),
        out_specs=(*[P("rep")] * 3, *[P("rep", "dp")] * 6),
        check_vma=False,
    )
```

time: 1820 us -> 1290 us (0.71)
  waiting for transfers between devices: 305 us -> 917 us
  starting transfers between devices: 517 us -> 0.37 us
  matrix products: 589 us -> 227 us
  other arithmetic: 267 us -> 8.88 us
    reduce_scatter x0 -> x6, waiting for transfers between devices: none -> 715 us  [body(): lax.psum_scatter(term.reshape(n * 400, 128), 'dp', scatter_dimension=0, t...]
    dot_general x198 -> x0, starting transfers between devices: 517 us -> none  [the longest x66 174 us: matmul(): jnp.dot(a, w, preferred_element_type=jnp.float32).astype(jnp.bfloat16)]
    dot_general x105 -> x15, matrix products: 589 us -> 227 us  [dot(): lax.dot_general(a, b, (((ca,), (cb,)), ((), ())), preferred_element_type=...]
    dot_general x192 -> x0, other arithmetic: 229 us -> none
    reshape x3 -> x0, waiting for transfers between devices: 202 us -> none  [step(): t.reshape(-1, *t.shape[2:])]
    all_gather x0 -> x3, waiting for transfers between devices: none -> 202 us  [body(): weights = [lax.all_gather(one[0], 'dp', axis=1, tiled=True) for one in new]]
    dot_general x198 -> x0, waiting for transfers between devices: 103 us -> none  [the longest x66 93 us: matmul(): jnp.dot(a, w, preferred_element_type=jnp.float32).astype(jnp.bfloat16)]
    reduce_sum x1 -> x0, blocking collectives: 38.4 us -> none  [of_a_group(): jnp.sum(g * g)]
  transfers between devices with their start and end apart: 201 -> 9, of which waited for: 39 -> 9; matrix products, arithmetic and copies ran while one was open for 41% -> 11% of each run, Pallas kernels for 0% -> 0%
where the time goes in v1:
time: 1290 us; the launch traced here: 1280 us
  waiting for transfers between devices  917 us (71%)
  matrix products  227 us (18%)
  local copies, waits for them, and re-layouts  70.5 us (5%)
  blocking collectives  37 us (3%)
  between operations  16.9 us (1%)
    reduce_scatter x6, waiting for transfers between devices, body(): lax.psum_scatter(term.reshape(n * 400, 128), 'dp', scatter_dimension=0, t...  715 us
    dot_general x15, matrix products, dot(): lax.dot_general(a, b, (((ca,), (cb,)), ((), ())), preferred_element_type=...  227 us
    all_gather x3, waiting for transfers between devices, body(): weights = [lax.all_gather(one[0], 'dp', axis=1, tiled=True) for one in new]  202 us
    psum x1, blocking collectives, body(): total = lax.psum(sum((jnp.sum(t * t) for t in g)), 'dp')  37 us
    reshape x6, local copies, waits for them, and re-layouts, body(): term.reshape(n * 400, 128)  34.6 us
    unnamed x37, local copies, waits for them, and re-layouts  28.1 us
  transfers between devices with their start and end apart: 9, of which 9 were waited for; matrix products, arithmetic and copies ran while one was open for 11% of the time, Pallas kernels for 0%

profile of v1, /device:TPU:0, one launch (start us, length us, event | category | flops | bytes accessed | tf_op | source)
XLA Modules:
  0.0 1278.0 jit_solution(544339804821413836)
XLA Ops:
  7.2 3.0 copy.37
  10.8 15.1 %fusion.42 = f32[2048,2560]{1,0:T(8,128)} fusion(bf16[2,640,2560]{2,1,0:T(8,128)(2,1)} %param.13, bf16[1,2048,640]{2,1,0:T(8,128)(2,1)} %param.11, f32[2048]{0:T(1024)S(1)} %add_rsqrt_fusion.1), kind=kOutput, calls=%fused_computation.55 | convolution fusion | flops 6714818560 | bytes 26877952 | tf_op jit(solution)/shard_map/dot_general | solution.py:11
  26.0 22.3 %multiply_convert_fusion.1 = (bf16[2048,2560]{1,0:T(8,128)(2,1)}, f32[2048,2560]{1,0:T(8,128)}) fusion(f32[2048,2560]{1,0:T(8,128)} %fusion.42, bf16[2,640,2560]{2,1,0:T(8,128)(2,1)} %param.14, bf16[1,2048,640]{2,1,0:T(8,128)(2,1)S(1)} %copy-done.6, f32[2048]{0:T(1024)S(1)} %add_rsqrt_fusion.1), kind=kOutput, calls=%fused_computation.13 | convolution fusion | flops 6746275840 | bytes 58335232 | tf_op jit(solution)/shard_map/dot_general | solution.py:11
  48.3 11.0 fusion.17
  59.3 14.4 %fusion.35 = f32[2048,2560]{1,0:T(8,128)} fusion(bf16[2,640,2560]{2,1,0:T(8,128)(2,1)} %param.14, bf16[2048,640]{0,1:T(8,128)(2,1)S(1)} %get-tuple-element.50, f32[2048]{0:T(1024)S(1)} %add_rsqrt_fusion), kind=kOutput, calls=%fused_computation.48 | convolution fusion | flops 6714818560 | bytes 26877952 | tf_op jit(solution)/shard_map/dot_general | solution.py:11
  73.6 13.4 %fusion.31 = f32[2048,2560]{1,0:T(8,128)} fusion(bf16[2,640,2560]{2,1,0:T(8,128)(2,1)} %param.13, bf16[2048,640]{0,1:T(8,128)(2,1)S(1)} %get-tuple-element.50, f32[2048]{0:T(1024)S(1)} %add_rsqrt_fusion), kind=kOutput, calls=%fused_computation.44 | convolution fusion | flops 6714818560 | bytes 26877952 | tf_op jit(solution)/shard_map/dot_general | solution.py:11
  87.0 3.0 copy.38
  90.0 29.3 %fusion.2 = (bf16[2048,2560]{1,0:T(8,128)(2,1)}, bf16[2048,2560]{1,0:T(8,128)(2,1)}) fusion(f32[2048,2560]{1,0:T(8,128)} %fusion.31, f32[2048,2560]{1,0:T(8,128)} %fusion.35, bf16[2,2560,640]{2,1,0:T(8,128)(2,1)} %param.15, bf16[1,2048,640]{2,1,0:T(8,128)(2,1)} %param.12), kind=kOutput, calls=%fused_computation.6 | convolution fusion | flops 6789529600 | bytes 68812800 | tf_op jit(solution)/shard_map/dot_general | solution.py:11
  119.3 10.8 fusion.51
  130.2 11.2 fusion.19
  141.4 1.8 fusion.64
  143.2 1.5 copy-done.5
  144.7 8.7 convolution_convert_fusion.2
  153.5 4.0 reshape.84
  157.5 18.6 %fusion.20 = bf16[2560,640]{1,0:T(8,128)(2,1)S(1)} fusion(f32[2048,2560]{1,0:T(8,128)} %fusion.35, f32[2048,2560]{1,0:T(8,128)} %fusion.31, bf16[1,2048,640]{2,1,0:T(8,128)(2,1)} %param.12), kind=kOutput, calls=%fused_computation.36 | convolution fusion | flops 6743982080 | bytes 47841280 | tf_op jit(solution)/shard_map/dot_general | solution.py:11
  176.1 4.0 reshape.85
  180.2 13.7 %convolution_convert_fusion = bf16[2048,2560]{1,0:T(8,128)(2,1)} fusion(bf16[2048,640]{0,1:T(8,128)(2,1)} %copy-done.5, bf16[2,2560,640]{2,1,0:T(8,128)(2,1)} %param.15), kind=kOutput, calls=%fused_computation.16 | convolution fusion | flops 6716129280 | bytes 16384000 | tf_op jit(solution)/shard_map/dot_general | solution.py:11
  193.9 15.2 %fusion.21 = bf16[640,2560]{1,0:T(8,128)(2,1)} fusion(bf16[2048,2560]{1,0:T(8,128)(2,1)} %convolution_convert_fusion, f32[2048,2560]{1,0:T(8,128)} %fusion.42, bf16[1,2048,640]{1,2,0:T(8,128)(2,1)S(1)} %copy-done.1, f32[2048]{0:T(1024)S(1)} %copy-done.10), kind=kOutput, calls=%fused_computation.37 | convolution fusion | flops 6753157120 | bytes 37363712 | tf_op jit(solution)/shard_map/dot_general | solution.py:11
  209.1 7.2 reshape.82
  216.5 12.0 convolution_convert_fusion.3
  228.5 7.3 reshape.83
  235.8 21.2 %fusion.24 = bf16[640,2560]{1,0:T(8,128)(2,1)} fusion(f32[2048,2560]{1,0:T(8,128)} %get-tuple-element.48, bf16[2048,2560]{1,0:T(8,128)(2,1)} %convolution_convert_fusion, f32[2048,2560]{1,0:T(8,128)} %fusion.42, bf16[1,2048,640]{1,2,0:T(8,128)(2,1)S(1)} %copy-done.1, f32[2048]{0:T(1024)S(1)} %copy-done.10), kind=kOutput, calls=%fused_computation.41 | convolution fusion | flops 6774128640 | bytes 58335232 | tf_op jit(solution)/shard_map/dot_general | solution.py:11
  257.1 7.3 reshape.80
  264.4 10.5 convolution_convert_fusion.4
  274.9 4.9 reshape.81
  279.8 21.1 %reduce-scatter.15.cloned.1.call-done = bf16[400,128]{1,0:T(8,128)(2,1)} async-done(((bf16[12800,128]{1,0:T(8,128)(2,1)}), bf16[400,128]{1,0:T(8,128)(2,1)}) %reduce-scatter.15.cloned.1.call-update) | async-done | bytes 102416 | tf_op jit(solution)/shard_map/reduce_scatter | solution.py:72
  301.9 138.9 %reduce-scatter.17.cloned.1.call-done = bf16[400,128]{1,0:T(8,128)(2,1)} async-done(((bf16[12800,128]{1,0:T(8,128)(2,1)}), bf16[400,128]{1,0:T(8,128)(2,1)}) %reduce-scatter.17.cloned.1.call-update) | async-done | bytes 102416 | tf_op jit(solution)/shard_map/reduce_scatter | solution.py:72
  441.7 138.9 %reduce-scatter.11.cloned.1.call-done = bf16[400,128]{1,0:T(8,128)(2,1)} async-done(((bf16[12800,128]{1,0:T(8,128)(2,1)}), bf16[400,128]{1,0:T(8,128)(2,1)}) %reduce-scatter.11.cloned.1.call-update) | async-done | bytes 102416 | tf_op jit(solution)/shard_map/reduce_scatter | solution.py:72
  580.7 1.0 stack_reshape.20
  581.7 139.3 %reduce-scatter.13.cloned.1.call-done = bf16[400,128]{1,0:T(8,128)(2,1)} async-done(((bf16[12800,128]{1,0:T(8,128)(2,1)}), bf16[400,128]{1,0:T(8,128)(2,1)}) %reduce-scatter.13.cloned.1.call-update) | async-done | bytes 102416 | tf_op jit(solution)/shard_map/reduce_scatter | solution.py:72
  721.0 1.0 stack_reshape.21
  722.0 139.2 %reduce-scatter.7.cloned.1.call-done = bf16[400,128]{1,0:T(8,128)(2,1)} async-done(((bf16[12800,128]{1,0:T(8,128)(2,1)}), bf16[400,128]{1,0:T(8,128)(2,1)}) %reduce-scatter.7.cloned.1.call-update) | async-done | bytes 102416 | tf_op jit(solution)/shard_map/reduce_scatter | solution.py:72
  861.2 1.0 stack_reshape.18
  863.7 137.8 %reduce-scatter.9.cloned.1.call-done = bf16[400,128]{1,0:T(8,128)(2,1)} async-done(((bf16[12800,128]{1,0:T(8,128)(2,1)}), bf16[400,128]{1,0:T(8,128)(2,1)}) %reduce-scatter.9.cloned.1.call-update) | async-done | bytes 102416 | tf_op jit(solution)/shard_map/reduce_scatter | solution.py:72
  1001.5 1.0 stack_reshape.19
  1005.2 37.0 %psum.7 = f32[]{:T(128)} all-reduce(f32[]{:T(128)S(6)} %add.123), channel_id=1, replica_groups=mesh['rep'=1,'dp'=32] {'dp'}, use_global_device_ids=true, to_apply=%region_12.13 | all-reduce | flops 1 | bytes 8 | tf_op jit(solution)/shard_map/psum | solution.py:75
  1042.9 2.3 fusion.99
  1045.3 2.0 fusion.86
  1049.1 1.1 copy.46
  1050.2 1.1 copy.47
  1051.3 1.1 copy.48
  1052.4 1.1 copy.49
  1053.4 62.8 %all-gather.8.cloned.1.call-done = bf16[2,2560,640]{2,1,0:T(8,128)(2,1)} async-done(((bf16[2,80,640]{2,1,0:T(8,128)(2,1)}), bf16[2,2560,640]{2,1,0:T(8,128)(2,1)}) %all-gather.8.cloned.1.call-update) | async-done | bytes 6553616 | tf_op jit(solution)/shard_map/all_gather | solution.py:82
  1116.2 72.9 %all-gather.4.cloned.1.call-done = bf16[2,640,2560]{2,0,1:T(2,128)(2,1)} async-done(((bf16[2,20,2560]{2,0,1:T(2,128)(2,1)}), bf16[2,640,2560]{2,0,1:T(2,128)(2,1)}) %all-gather.4.cloned.1.call-update) | async-done | bytes 6553616 | tf_op jit(solution)/shard_map/all_gather | solution.py:82
  1189.1 6.7 copy.44
  1195.8 65.9 %all-gather.6.cloned.1.call-done = bf16[2,640,2560]{2,0,1:T(2,128)(2,1)} async-done(((bf16[2,20,2560]{2,0,1:T(2,128)(2,1)}), bf16[2,640,2560]{2,0,1:T(2,128)(2,1)}) %all-gather.6.cloned.1.call-update) | async-done | bytes 6553616 | tf_op jit(solution)/shard_map/all_gather | solution.py:82
  1261.7 6.8 copy.45
  1268.5 2.8 copy.67
  (57 shorter events, 7.0 us)
Async XLA Ops:
  7.2 293.7 %reduce-scatter.15.cloned.1.call-start = ((), (), s32[]{:S(2)}) async-start(), calls=%async_computation.10 | async-start | bytes 3379200 | tf_op jit(solution)/shard_map/reduce_scatter | solution.py:72
  10.2 38.0 %copy-start = (bf16[1,2048,640]{1,2,0:T(8,128)(2,1)}, bf16[1,2048,640]{1,2,0:T(8,128)(2,1)S(1)}, u32[]{:S(2)}) copy-start(bf16[1,2048,640]{1,2,0:T(8,128)(2,1)S(1)} %copy.37) | copy-start | bytes 7864324
  10.8 15.2 %copy-start.9 = (f32[2048]{0:T(1024)}, f32[2048]{0:T(1024)S(1)}, u32[]{:S(2)}) copy-start(f32[2048]{0:T(1024)S(1)} %add_rsqrt_fusion.1) | copy-start | bytes 24580
  10.8 15.2 %copy-start.6 = (bf16[1,2048,640]{2,1,0:T(8,128)(2,1)S(1)}, bf16[1,2048,640]{2,1,0:T(8,128)(2,1)}, u32[]{:S(2)}) copy-start(bf16[1,2048,640]{2,1,0:T(8,128)(2,1)} %param.11) | copy-start | bytes 7864324
  59.3 14.4 %copy-start.3 = (bf16[2048,640]{0,1:T(8,128)(2,1)}, bf16[2048,640]{0,1:T(8,128)(2,1)S(1)}, u32[]{:S(2)}) copy-start(bf16[2048,640]{0,1:T(8,128)(2,1)S(1)} %get-tuple-element.50) | copy-start | bytes 7864324
  119.3 10.8 copy-start.4
  130.1 14.6 %slice-start = ((s8[10485760]{0:T(1024)(128)(4,1)}), s8[4194304]{0:T(1024)(128)(4,1)S(1)}, s32[]{:S(2)}) async-start(s8[10485760]{0:T(1024)(128)(4,1)} %bitcast.72), calls=%async_computation.15 | async-start | bytes 8388608
  130.1 14.6 %slice-start.1 = ((s8[10485760]{0:T(1024)(128)(4,1)}), s8[4194304]{0:T(1024)(128)(4,1)S(1)}, s32[]{:S(2)}) async-start(s8[10485760]{0:T(1024)(128)(4,1)} %bitcast.72), calls=%async_computation.16 | async-start | bytes 8388608
  130.1 14.6 %slice-start.2 = ((s8[10485760]{0:T(1024)(128)(4,1)}), s8[2097152]{0:T(1024)(128)(4,1)S(1)}, s32[]{:S(2)}) async-start(s8[10485760]{0:T(1024)(128)(4,1)} %bitcast.72), calls=%async_computation.17 | async-start | bytes 4194304
  143.2 1.5 copy-start.5
  157.4 283.3 %reduce-scatter.17.cloned.1.call-start = ((), (), s32[]{:S(2)}) async-start(), calls=%async_computation.11 | async-start | bytes 3379200 | tf_op jit(solution)/shard_map/reduce_scatter | solution.py:72
  180.2 13.8 %copy-start.1 = (bf16[1,2048,640]{1,2,0:T(8,128)(2,1)S(1)}, bf16[1,2048,640]{1,2,0:T(8,128)(2,1)}, u32[]{:S(2)}) copy-start(bf16[1,2048,640]{1,2,0:T(8,128)(2,1)} %copy-done) | copy-start | bytes 7864324
  180.2 13.8 %copy-start.10 = (f32[2048]{0:T(1024)S(1)}, f32[2048]{0:T(1024)}, u32[]{:S(2)}) copy-start(f32[2048]{0:T(1024)} %copy-done.9) | copy-start | bytes 24580
  180.2 400.5 %reduce-scatter.11.cloned.1.call-start = ((), (), s32[]{:S(2)}) async-start(), calls=%async_computation.8 | async-start | bytes 3379200 | tf_op jit(solution)/shard_map/reduce_scatter | solution.py:72
  216.4 504.6 %reduce-scatter.13.cloned.1.call-start = ((), (), s32[]{:S(2)}) async-start(), calls=%async_computation.9 | async-start | bytes 3379200 | tf_op jit(solution)/shard_map/reduce_scatter | solution.py:72
  235.8 625.5 %reduce-scatter.7.cloned.1.call-start = ((), (), s32[]{:S(2)}) async-start(), calls=%async_computation.6 | async-start | bytes 3379200 | tf_op jit(solution)/shard_map/reduce_scatter | solution.py:72
  264.3 737.2 %reduce-scatter.9.cloned.1.call-start = ((), (), s32[]{:S(2)}) async-start(), calls=%async_computation.7 | async-start | bytes 3379200 | tf_op jit(solution)/shard_map/reduce_scatter | solution.py:72
  279.7 765.6 %copy-start.7 = (f32[2,20,2560]{2,0,1:T(2,128)S(1)}, f32[2,20,2560]{2,0,1:T(2,128)}, u32[]{:S(2)}) copy-start(f32[2,20,2560]{2,0,1:T(2,128)} %param.19) | copy-start | bytes 1228804
  279.8 765.6 %copy-start.8 = (f32[2,20,2560]{2,0,1:T(2,128)S(1)}, f32[2,20,2560]{2,0,1:T(2,128)}, u32[]{:S(2)}) copy-start(f32[2,20,2560]{2,0,1:T(2,128)} %param.16) | copy-start | bytes 1228804
  279.8 836.5 %all-gather.8.cloned.1.call-start = ((), (), s32[]{:S(2)}) async-start(), calls=%async_computation.14 | async-start | bytes 6758400 | tf_op jit(solution)/shard_map/all_gather | solution.py:82
  1045.3 143.8 %all-gather.4.cloned.1.call-start = ((), (), s32[]{:S(2)}) async-start(), calls=%async_computation.12 | async-start | bytes 6758400 | tf_op jit(solution)/shard_map/all_gather | solution.py:82
  1048.2 213.4 %all-gather.6.cloned.1.call-start = ((), (), s32[]{:S(2)}) async-start(), calls=%async_computation.13 | async-start | bytes 6758400 | tf_op jit(solution)/shard_map/all_gather | solution.py:82
  1261.7 6.8 copy-start.2
Sparse Core Ops, SparseCore 0:
  157.6 143.2 reduce-scatter.14
  303.2 137.5 reduce-scatter.16
  443.1 137.5 reduce-scatter.10
  583.4 137.5 reduce-scatter.12
  723.7 137.5 reduce-scatter.6
  864.0 137.4 reduce-scatter.8
  1045.4 70.8 all-gather.7
  1119.7 69.3 all-gather.3
  1192.5 69.0 all-gather.5

commit v2 on v1

v2 whole, which is shorter than its diff:
```python
import functools

import jax
import jax.numpy as jnp
from jax import lax
from jax.experimental import pallas as pl
from jax.experimental.pallas import tpu as pltpu
from jax.sharding import PartitionSpec as P

F32, BF16 = jnp.float32, jnp.bfloat16


def dot(a, b, ca, cb):
    return lax.dot_general(a, b, (((ca,), (cb,)), ((), ())), preferred_element_type=F32)


def norm_scale(h):
    wide = h.astype(F32)
    return wide, lax.rsqrt(jnp.mean(wide**2, -1, keepdims=True) + 1e-6)


def hidden(a, wg, wu):
    gate, up = dot(a, wg, 1, 0), dot(a, wu, 1, 0)
    return gate, up, (jax.nn.silu(gate) * up).astype(BF16)


def hidden_back(ds, gate, up):
    ds = ds.astype(F32)
    sig = jax.nn.sigmoid(gate)
    d_up = (ds * (gate * sig)).astype(BF16)
    d_gate = (ds * up * (sig * (1 + gate * (1 - sig)))).astype(BF16)
    return d_gate, d_up


def gradients(x, dy, wg, wu, wd):
    wide0, r0 = norm_scale(x)
    a1 = (wide0 * r0).astype(BF16)
    gate1, up1, s1 = hidden(a1, wg[0], wu[0])
    h1 = x + dot(s1, wd[0], 1, 0).astype(BF16)
    wide1, r1 = norm_scale(h1)
    a2 = (wide1 * r1).astype(BF16)
    gate2, up2, s2 = hidden(a2, wg[1], wu[1])

    ds2 = dot(dy, wd[1], 1, 1).astype(BF16)
    d_gate2, d_up2 = hidden_back(ds2, gate2, up2)
    da2 = (dot(d_gate2, wg[1], 1, 1).astype(BF16) + dot(d_up2, wu[1], 1, 1).astype(BF16)).astype(F32)
    back = da2 * r1 - wide1 * (r1**3 * jnp.mean(da2 * wide1, -1, keepdims=True))
    dh1 = dy + back.astype(BF16)
    ds1 = dot(dh1, wd[0], 1, 1).astype(BF16)
    d_gate1, d_up1 = hidden_back(ds1, gate1, up1)

    terms = ((a1, d_gate1), (a1, d_up1), (s1, dh1)), ((a2, d_gate2), (a2, d_up2), (s2, dy))
    return [[dot(a, b, 0, 0).astype(BF16) for a, b in layer] for layer in terms]


MESH = pl.DeviceIdType.MESH
MATRICES = (("d", 0, 1, 2), ("w", 0, 1, 0), ("w", 1, 1, 1), ("d", 1, 0, 2), ("w", 2, 0, 0), ("w", 3, 0, 1))
SIX = range(6)


def step_kernel(count, *refs):
    terms, weights, moments, out_w, out_m = refs[0:6], refs[6:9], refs[9:15], refs[15:18], refs[18:24]
    own_w, own_d, two_w, two_d, r1_w, r1_d, r2_w, r2_d, zl_w, zl_d, zr_w, zr_d = refs[24:36]
    tmp_w, tmp_d, g_w, g_d, state_w, state_d, old_w, old_d, new_w, got_w, norm = refs[36:47]
    (loc_sem, aux_sem, two_s, two_r, s1_s, s1_r, s2_s, s2_r, z_s, zl_r, zr_r, g_s, g_r, n_s, n_r, nz_r, w_s, w_r, ag_r, agz_s, ag1_s, ag2_s,
     ag3_s, agt_s, agt_r, out_s, out2_s) = refs[47:74]
    own, two = {"w": own_w, "d": own_d}, {"w": two_w, "d": two_d}
    r1, r2 = {"w": r1_w, "d": r1_d}, {"w": r2_w, "d": r2_d}
    zl, zr, tmp = {"w": zl_w, "d": zl_d}, {"w": zr_w, "d": zr_d}, {"w": tmp_w, "d": tmp_d}

    me = lax.axis_index("dp")
    core, z, y, x = lax.rem(me, 2), lax.rem(me // 2, 4), lax.rem(me // 8, 2), me // 16
    half = own_w.shape[-1]

    def device(x, y, z, core):
        return {"dp": ((x * 2 + y) * 4 + z) * 2 + core}

    partner = device(x, y, z, 1 - core)
    by_x, by_y = device(1 - x, y, z, core), device(x, 1 - y, z, core)
    right, left = device(x, y, z + 1, core), device(x, y, z - 1, core)
    line = [device(x, y, lax.rem(z + o, 4), core) for o in (1, 2, 3)]

    def columns(c):
        return pl.ds(pl.multiple_of(c * half, 128), half)

    def remote(src, dst, send, recv, to):
        return pltpu.make_async_remote_copy(src_ref=src, dst_ref=dst, send_sem=send, recv_sem=recv, device_id=to, device_id_type=MESH)

    barrier = pltpu.get_barrier_semaphore()
    for other in (partner, by_x, by_y, *line):
        pl.semaphore_signal(barrier, inc=1, device_id=other, device_id_type=MESH)
    pl.semaphore_wait(barrier, 6)

    def half_of(j, c):
        return terms[j].at[:, :, :, columns(c)] if MATRICES[j][0] == "w" else terms[j].at[:, :, c]

    def to_partner(j):
        kind, t, _, _ = MATRICES[j]
        return remote(half_of(j, 1 - core), two[kind].at[t], two_s.at[j], two_r.at[j], partner)

    def bring(j):
        kind, t, _, _ = MATRICES[j]
        return pltpu.make_async_copy(half_of(j, core), own[kind].at[t], loc_sem.at[j])

    for j in SIX:
        to_partner(j).start()
        bring(j).start()
    chip = (x * 2 + y, z)
    aux = [pltpu.make_async_copy(moments[i], (state_w, state_w, state_w, state_w, state_d, state_d)[i].at[(0, 1, 2, 3, 0, 1)[i]], aux_sem.at[i]) for i in SIX]
    aux += [pltpu.make_async_copy(weights[i].at[:, chip[0], chip[1]], old_w.at[i], aux_sem.at[6 + i]) for i in range(2)]
    aux += [pltpu.make_async_copy(weights[2].at[:, chip[0], chip[1], core], old_d, aux_sem.at[8])]
    for copy in aux:
        copy.start()

    def add_into(out, *parts):
        total = parts[0][...].astype(F32)
        for part in parts[1:]:
            total = total + part[...].astype(F32)
        out[...] = total.astype(out.dtype)

    def x_first(j):
        return j % 2 == 0

    def first(j, i):
        kind, t, _, _ = MATRICES[j]
        group = (1 - x) * 2 + i if x_first(j) else i * 2 + (1 - y)
        return group, remote(own[kind].at[t, group], r1[kind].at[t, i], s1_s.at[j, i], s1_r.at[j, i], by_x if x_first(j) else by_y)

    def second(j):
        kind, t, _, _ = MATRICES[j]
        group, i = (x * 2 + (1 - y), 1 - y) if x_first(j) else ((1 - x) * 2 + y, 1 - x)
        return group, i, remote(own[kind].at[t, group], r2[kind].at[t], s2_s.at[j], s2_r.at[j], by_y if x_first(j) else by_x)

    def along(j, to, rightward):
        kind, t, _, _ = MATRICES[j]
        land, sems = (zl, zl_r) if rightward else (zr, zr_r)
        return remote(own[kind].at[t, chip[0], to], land[kind].at[t, to], z_s.at[j, to], sems.at[j, to], right if rightward else left)

    for j in SIX:
        kind, t, _, _ = MATRICES[j]
        to_partner(j).wait_recv()
        bring(j).wait()
        for i in range(2):
            group, copy = first(j, i)

            @pl.loop(0, 4)
            def _(b):
                add_into(own[kind].at[t, group, b], own[kind].at[t, group, b], two[kind].at[t, group, b])

            copy.start()
    for j in SIX:
        kind, t, _, _ = MATRICES[j]
        for i in range(2):
            first(j, i)[1].wait_recv()
        group, i, copy = second(j)

        @pl.loop(0, 4)
        def _(b):
            add_into(own[kind].at[t, group, b], own[kind].at[t, group, b], two[kind].at[t, group, b], r1[kind].at[t, i, b])

        copy.start()

    def partial(j, to):
        kind, t, _, _ = MATRICES[j]
        add_into(tmp[kind], own[kind].at[t, chip[0], to], two[kind].at[t, chip[0], to], r1[kind].at[t, y if x_first(j) else x, to], r2[kind].at[t, to])

    def add_landed(j, to, rightward):
        kind, t, _, _ = MATRICES[j]
        along(j, to, rightward).wait_recv()
        land = zl if rightward else zr
        add_into(tmp[kind], tmp[kind], land[kind].at[t, to])

    def pass_on(j, to, rightward):
        kind, t, _, _ = MATRICES[j]
        partial(j, to)

        @pl.when(z > 0 if rightward else z < 3)
        def _():
            add_landed(j, to, rightward)

        own[kind][t, chip[0], to] = tmp[kind][...].astype(BF16)
        along(j, to, rightward).start()

    squares = None
    for j in SIX:
        second(j)[2].wait_recv()
        for to in range(3):

            @pl.when(3 - to > z)
            def _():
                pass_on(j, 3 - to, True)

            @pl.when(to < z)
            def _():
                pass_on(j, to, False)

    for j in SIX:
        kind, t, _, _ = MATRICES[j]
        partial(j, z)

        @pl.when(z > 0)
        def _():
            add_landed(j, z, True)

        @pl.when(z < 3)
        def _():
            add_landed(j, z, False)

        total = tmp[kind][...].astype(BF16)
        if kind == "w":
            g_w[t, core] = total
            remote(g_w.at[t, core], g_w.at[t, core], g_s.at[t], g_r.at[t], partner).start()
        else:
            g_d[t] = total
        wide = total.astype(F32)
        for r in range(0, wide.shape[0], 8):
            for c in range(0, wide.shape[1], 128):
                part = wide[r : r + 8, c : c + 128]
                squares = part * part if squares is None else squares + part * part

    for j in SIX:
        to_partner(j).wait_send()
        for i in range(2):
            first(j, i)[1].wait_send()
        second(j)[2].wait_send()
        for to in range(4):

            @pl.when(to != z)
            def _():
                along(j, to, True).wait_send()

    norm[0] = squares
    for s, other in enumerate((partner, by_x, by_y)):
        copy = remote(norm.at[2 * s], norm.at[2 * s + 1], n_s.at[s], n_r.at[s], other)
        copy.start()
        copy.wait()
        norm[2 * s + 2] = norm[2 * s] + norm[2 * s + 1]
    norm[7 + z] = norm[6]
    for o in range(3):
        remote(norm.at[6], norm.at[7 + z], n_s.at[3 + o], nz_r.at[z], line[o]).start()
    for o in range(3):
        there = lax.rem(z + o + 1, 4)
        remote(norm.at[6], norm.at[7 + there], n_s.at[3 + o], nz_r.at[there], line[o]).wait()
    total = (norm[7] + norm[8]) + (norm[9] + norm[10])
    total = jnp.sum(jnp.sum(total, axis=1, keepdims=True), axis=0, keepdims=True)
    factor = jnp.minimum(1.0, 0.5 * lax.rsqrt(total / count + 1e-30))

    def update(w, m, v, g):
        g = g.astype(F32) * factor
        m = 0.9 * m + 0.1 * g
        v = 0.95 * v + 0.05 * g * g
        step = m * lax.rsqrt(v + 1e-8) + 0.1 * w.astype(F32)
        return (w.astype(F32) - 0.02 * step).astype(BF16), m, v

    for copy in aux:
        copy.wait()

    def swap(t):
        return remote(new_w.at[t, 1 - core], got_w.at[t], w_s.at[t], w_r.at[t], partner)

    for t in range(4):
        arg, layer = t % 2, 1 - t // 2
        theirs = remote(g_w.at[t, 1 - core], g_w.at[t, 1 - core], g_s.at[t], g_r.at[t], partner)
        theirs.wait_recv()
        for h in range(2):
            cut = slice(h * half, (h + 1) * half)
            w, m, v = update(old_w[arg, layer, :, cut], state_w[arg, layer, :, cut], state_w[2 + arg, layer, :, cut], g_w[t, h])
            new_w[t, h], state_w[arg, layer, :, cut], state_w[2 + arg, layer, :, cut] = w, m, v
        swap(t).start()
    for t in range(2):
        layer = 1 - t
        w, m, v = update(old_d[layer], state_d[0, layer], state_d[1, layer], g_d[t])
        own_d[t, chip[0], z], state_d[0, layer], state_d[1, layer] = w, m, v
    for t in range(4):
        swap(t).wait_recv()
        rows = lax.broadcasted_iota(jnp.int32, tmp_w.shape, 0)
        mine = (rows < tmp_w.shape[0] // 2) == (core == 0)
        own_w[t, chip[0], z] = jnp.where(mine, new_w[t, core].astype(F32), got_w[t].astype(F32)).astype(BF16)
    back = [pltpu.make_async_copy((state_w, state_w, state_w, state_w, state_d, state_d)[i].at[(0, 1, 2, 3, 0, 1)[i]], out_m[i], aux_sem.at[i]) for i in SIX]
    for copy in back:
        copy.start()

    def spread(j, group, zs, sem, to):
        kind, t, _, _ = MATRICES[j]
        place = own[kind].at[t, group, zs]
        return remote(place, place, sem, ag_r.at[j, group, zs], to)

    def near(j):
        return by_y if x_first(j) else by_x

    def far(j):
        return by_x if x_first(j) else by_y

    def groups(j):
        a, b = x * 2 + (1 - y), (1 - x) * 2 + y
        return (x * 2 + y, *((a, b) if x_first(j) else (b, a)), (1 - x) * 2 + (1 - y))

    def sideways(j, zs):
        spread(j, chip[0], zs, ag2_s.at[j, zs], far(j)).start()
        spread(j, chip[0], zs, ag1_s.at[j, zs], near(j)).start()

    def arrived(j, group, zs):
        spread(j, group, zs, ag1_s.at[j, zs], partner).wait_recv()

    def onward(j, zs):
        arrived(j, groups(j)[1], zs)
        spread(j, groups(j)[1], zs, ag3_s.at[j, zs], far(j)).start()

    for j in SIX:

        @pl.when(z < 3)
        def _():
            spread(j, chip[0], z, agz_s.at[j, z, 0], right).start()

        @pl.when(z > 0)
        def _():
            spread(j, chip[0], z, agz_s.at[j, z, 1], left).start()

        sideways(j, z)
    for d in (1, 2, 3, 4):
        for j in SIX:
            if d < 4:

                @pl.when(z - d >= 0)
                def _():
                    arrived(j, chip[0], z - d)

                    @pl.when(z < 3)
                    def _():
                        spread(j, chip[0], z - d, agz_s.at[j, z - d, 0], right).start()

                    sideways(j, z - d)

                @pl.when(z + d <= 3)
                def _():
                    arrived(j, chip[0], z + d)

                    @pl.when(z > 0)
                    def _():
                        spread(j, chip[0], z + d, agz_s.at[j, z + d, 1], left).start()

                    sideways(j, z + d)

            if d == 1:
                onward(j, z)
            else:

                @pl.when(z - (d - 1) >= 0)
                def _():
                    onward(j, z - (d - 1))

                @pl.when(z + (d - 1) <= 3)
                def _():
                    onward(j, z + (d - 1))

    def across(j, i):
        kind, t, _, _ = MATRICES[j]
        group = groups(j)[i]
        return group, remote(own[kind].at[t, group], two[kind].at[t, group], agt_s.at[j, i], agt_r.at[j, group], partner)

    def put(j, group, c, buffer, sem):
        kind, t, layer, arg = MATRICES[j]
        to = out_w[arg].at[layer, group, :, :, columns(c)] if kind == "w" else out_w[arg].at[layer, group, :, c]
        return pltpu.make_async_copy(buffer[kind].at[t, group], to, sem)

    for i in range(4):
        for j in SIX:
            if i >= 2:
                for zs in range(4):
                    arrived(j, groups(j)[i], zs)
            group, copy = across(j, i)
            copy.start()
            put(j, group, core, own, out_s.at[j, i]).start()
        if i:
            for j in SIX:
                group, copy = across(j, i - 1)
                copy.wait_recv()
                put(j, group, 1 - core, two, out2_s.at[j, i - 1]).start()
    for j in SIX:
        group, copy = across(j, 3)
        copy.wait_recv()
        put(j, group, 1 - core, two, out2_s.at[j, 3]).start()

    for copy in back:
        copy.wait()
    for t in range(4):
        remote(g_w.at[t, core], g_w.at[t, core], g_s.at[t], g_r.at[t], partner).wait_send()
        swap(t).wait_send()
    for j in SIX:
        for zs in range(4):
            spread(j, chip[0], zs, ag1_s.at[j, zs], near(j)).wait_send()
            spread(j, chip[0], zs, ag2_s.at[j, zs], far(j)).wait_send()
            spread(j, chip[0], zs, ag3_s.at[j, zs], far(j)).wait_send()

            @pl.when(jnp.logical_and(zs <= z, z < 3))
            def _():
                spread(j, chip[0], zs, agz_s.at[j, zs, 0], right).wait_send()

            @pl.when(jnp.logical_and(zs >= z, z > 0))
            def _():
                spread(j, chip[0], zs, agz_s.at[j, zs, 1], left).wait_send()

        for i in range(4):
            group, copy = across(j, i)
            copy.wait_send()
            put(j, group, core, own, out_s.at[j, i]).wait()
            put(j, group, 1 - core, two, out2_s.at[j, i]).wait()


def reduce_step_gather(terms, weights, moments):
    wide = next(t for t, m in zip(terms, MATRICES) if m[0] == "w").shape
    down = terms[0].shape
    rw, cw, rd, cd = wide[2], wide[3] // 2, down[3], down[4]
    count = 4 * 16 * rw * 2 * cw + 2 * 32 * rd * cd
    vm, dma = pltpu.VMEM, pltpu.SemaphoreType.DMA
    w, d = (rw, cw), (rd, cd)
    scratch = [
        vm((4, 4, 4, *w), BF16), vm((2, 4, 4, *d), BF16), vm((4, 4, 4, *w), BF16), vm((2, 4, 4, *d), BF16),
        vm((4, 2, 4, *w), BF16), vm((2, 2, 4, *d), BF16), vm((4, 4, *w), BF16), vm((2, 4, *d), BF16),
        vm((4, 4, *w), BF16), vm((2, 4, *d), BF16), vm((4, 4, *w), BF16), vm((2, 4, *d), BF16),
        vm(w, F32), vm(d, F32), vm((4, 2, *w), BF16), vm((2, *d), BF16),
        vm((4, 2, rw, 2 * cw), F32), vm((2, 2, *d), F32), vm((2, 2, rw, 2 * cw), BF16), vm((2, *d), BF16),
        vm((4, 2, *w), BF16), vm((4, *w), BF16), vm((11, 8, 128), F32),
        dma((6,)), dma((9,)), dma((6,)), dma((6,)), dma((6, 2)), dma((6, 2)), dma((6,)), dma((6,)), dma((6, 4)), dma((6, 4)), dma((6, 4)),
        dma((4,)), dma((4,)), dma((6,)), dma((3,)), dma((4,)), dma((4,)), dma((4,)),
        dma((6, 4, 4)), dma((6, 4, 2)), dma((6, 4)), dma((6, 4)), dma((6, 4)), dma((6, 4)), dma((6, 4)), dma((6, 4)), dma((6, 4)),
    ]
    outs = [jax.ShapeDtypeStruct(a.shape, a.dtype) for a in (*weights, *moments)]
    return pl.pallas_call(
        functools.partial(step_kernel, count),
        out_shape=outs,
        in_specs=[pl.BlockSpec(memory_space=pl.ANY)] * 15,
        out_specs=[pl.BlockSpec(memory_space=pl.ANY)] * 9,
        scratch_shapes=scratch,
        compiler_params=pltpu.CompilerParams(collective_id=0, has_side_effects=True, vmem_limit_bytes=60 * 2**20),
        name="reduce_step_gather",
    )(*terms, *weights, *moments)


def all_steps(me, terms, w, m, v):
    core = me % 2

    def blocks(t):
        return t.reshape(*t.shape[:-2], 4, 4, t.shape[-2] // 16, t.shape[-1])

    def down_blocks(t):
        return t.reshape(*t.shape[:-2], 4, 4, 2, t.shape[-2] // 32, t.shape[-1])

    ordered = [(blocks if kind == "w" else down_blocks)(terms[layer][arg]) for kind, _, layer, arg in MATRICES]
    twice = [jnp.concatenate([t, t], axis=1) for t in (m[0], m[1], v[0], v[1])]
    weights = [blocks(w[0]), blocks(w[1]), down_blocks(w[2])]
    out = reduce_step_gather(ordered, weights, [*twice, m[2], v[2]])
    new = [a.reshape(b.shape) for a, b in zip(out[:3], w)]
    rows = m[0].shape[1]
    mine = [jnp.where(core == 0, t[:, :rows], t[:, rows:]) for t in out[3:7]]
    return (*new, mine[0], mine[1], out[7], mine[2], mine[3], out[8])


def solution(mesh):
    def body(x, dy, *arrays):
        w, m, v = (arrays[i : i + 3] for i in (0, 3, 6))
        return all_steps(lax.axis_index("dp"), gradients(x[0], dy[0], *w), w, m, v)

    moments = P(None, "dp", None)
    return jax.shard_map(
        body,
        mesh=mesh,
        in_specs=(P(("rep", "dp")), P(("rep", "dp")), *[P()] * 3, *[moments] * 6),
        out_specs=(*[P("rep")] * 3, *[P("rep", "dp")] * 6),
        check_vma=False,
    )
```

time: 1290 us -> 513 us (0.40)
  waiting for transfers between devices: 917 us -> 0 us
  Pallas kernels: 0 us -> 242 us
  local copies, waits for them, and re-layouts: 70.5 us -> 23.3 us
  blocking collectives: 37 us -> 0 us
  between operations: 16.9 us -> 1.39 us
    reduce_scatter x6 -> x0, waiting for transfers between devices: 715 us -> none  [body(): lax.psum_scatter(term.reshape(n * 400, 128), 'dp', scatter_dimension=0, t...]
    pallas_call x0 -> x1, Pallas kernels: none -> 242 us  [reduce_step_gather(): pl.pallas_call(functools.partial(step_kernel, count), out_shape=outs, in_...]
    all_gather x3 -> x0, waiting for transfers between devices: 202 us -> none  [body(): weights = [lax.all_gather(one[0], 'dp', axis=1, tiled=True) for one in new]]
    psum x1 -> x0, blocking collectives: 37 us -> none  [body(): total = lax.psum(sum((jnp.sum(t * t) for t in g)), 'dp')]
    reshape x6 -> x0, local copies, waits for them, and re-layouts: 34.6 us -> none  [body(): term.reshape(n * 400, 128)]
    unnamed x37 -> x71, local copies, waits for them, and re-layouts: 28.1 us -> 23.3 us
  transfers between devices with their start and end apart: 9 -> 0, of which waited for: 9 -> 0; matrix products, arithmetic and copies ran while one was open for 11% -> 0% of each run, Pallas kernels for 0% -> 0%
where the time goes in v2:
time: 513 us; the launch traced here: 505 us
  Pallas kernels  242 us (47%)
  matrix products  226 us (44%)
  local copies, waits for them, and re-layouts  23.3 us (5%)
  other arithmetic  12.5 us (2%)
    pallas_call x1, Pallas kernels, reduce_step_gather(): pl.pallas_call(functools.partial(step_kernel, count), out_shape=outs, in_...  242 us
    dot_general x15, matrix products, dot(): lax.dot_general(a, b, (((ca,), (cb,)), ((), ())), preferred_element_type=...  226 us
    unnamed x71, local copies, waits for them, and re-layouts  23.3 us

profile of v2, /device:TPU:0, one launch (start us, length us, event | category | flops | bytes accessed | tf_op | source)
XLA Modules:
  0.0 505.3 jit_solution(16557098434236884249)
XLA Ops:
  0.6 3.0 copy.20
  3.7 0.0 slice-start
  3.7 0.6 fusion.13
  4.2 0.0 slice-start.1
  4.3 16.1 %fusion.43 = f32[2048,2560]{1,0:T(8,128)} fusion(bf16[2,640,2560]{2,1,0:T(8,128)(2,1)} %param.13, bf16[1,2048,640]{2,1,0:T(8,128)(2,1)} %param.11, f32[2048]{0:T(1024)S(1)} %add_rsqrt_fusion.1), kind=kOutput, calls=%fused_computation.56 | convolution fusion | flops 6714818560 | bytes 26877952 | tf_op jit(solution)/shard_map/dot_general | solution.py:14
  20.4 21.4 %multiply_convert_fusion.1 = (bf16[2048,2560]{1,0:T(8,128)(2,1)}, f32[2048,2560]{1,0:T(8,128)}) fusion(f32[2048,2560]{1,0:T(8,128)} %fusion.43, bf16[2,640,2560]{2,1,0:T(8,128)(2,1)S(1)} %bitcast.86, bf16[1,2048,640]{2,1,0:T(8,128)(2,1)} %param.11, f32[2048]{0:T(1024)S(1)} %add_rsqrt_fusion.1), kind=kOutput, calls=%fused_computation.13 | convolution fusion | flops 6746275840 | bytes 58335232 | tf_op jit(solution)/shard_map/dot_general | solution.py:14
  41.8 11.0 %fusion.17 = (f32[2048]{0:T(1024)S(1)}, bf16[2048,640]{0,1:T(8,128)(2,1)S(1)}) fusion(bf16[2048,2560]{1,0:T(8,128)(2,1)} %get-tuple-element.38, bf16[2,2560,640]{2,1,0:T(8,128)(2,1)} %param.15, bf16[1,2048,640]{1,2,0:T(8,128)(2,1)S(1)} %copy.20), kind=kOutput, calls=%fused_computation.32 | convolution fusion | flops 6717437952 | bytes 19013632 | tf_op jit(solution)/shard_map/dot_general | solution.py:14
  52.8 0.0 copy-start.12
  52.8 11.7 %fusion.32 = f32[2048,2560]{1,0:T(8,128)} fusion(bf16[2,640,2560]{2,1,0:T(8,128)(2,1)S(1)} %bitcast.86, bf16[2048,640]{0,1:T(8,128)(2,1)S(1)} %get-tuple-element.41, f32[2048]{0:T(1024)S(1)} %add_rsqrt_fusion), kind=kOutput, calls=%fused_computation.45 | convolution fusion | flops 6714818560 | bytes 26877952 | tf_op jit(solution)/shard_map/dot_general | solution.py:14
  64.5 13.6 %fusion.36 = f32[2048,2560]{1,0:T(8,128)} fusion(bf16[2,640,2560]{2,1,0:T(8,128)(2,1)} %param.13, bf16[2048,640]{0,1:T(8,128)(2,1)S(1)} %get-tuple-element.41, f32[2048]{0:T(1024)S(1)} %add_rsqrt_fusion), kind=kOutput, calls=%fused_computation.49 | convolution fusion | flops 6714818560 | bytes 26877952 | tf_op jit(solution)/shard_map/dot_general | solution.py:14
  78.1 19.1 %fusion.20 = bf16[2560,640]{1,0:T(8,128)(2,1)} fusion(f32[2048,2560]{1,0:T(8,128)} %fusion.32, f32[2048,2560]{1,0:T(8,128)} %fusion.36, bf16[1,2048,640]{2,1,0:T(8,128)(2,1)S(1)} %copy-done.5), kind=kOutput, calls=%fused_computation.36 | convolution fusion | flops 6743982080 | bytes 47841280 | tf_op jit(solution)/shard_map/dot_general | solution.py:14
  97.1 29.9 %fusion.2 = (bf16[2048,2560]{1,0:T(8,128)(2,1)}, bf16[2048,2560]{1,0:T(8,128)(2,1)}) fusion(f32[2048,2560]{1,0:T(8,128)} %fusion.36, f32[2048,2560]{1,0:T(8,128)} %fusion.32, bf16[2,2560,640]{2,1,0:T(8,128)(2,1)} %param.15, bf16[1,2048,640]{2,1,0:T(8,128)(2,1)} %param.12), kind=kOutput, calls=%fused_computation.6 | convolution fusion | flops 6789529600 | bytes 68812800 | tf_op jit(solution)/shard_map/dot_general | solution.py:14
  127.1 0.0 slice-start.2
  127.1 10.9 %convolution_convert_fusion.4 = bf16[640,2560]{1,0:T(8,128)(2,1)} fusion(bf16[2048,2560]{1,0:T(8,128)(2,1)} %get-tuple-element.37, bf16[2048,640]{0,1:T(8,128)(2,1)S(1)} %copy-done.4, f32[2048]{0:T(1024)S(1)} %add_rsqrt_fusion), kind=kOutput, calls=%fused_computation.40 | convolution fusion | flops 6716456960 | bytes 16392192 | tf_op jit(solution)/shard_map/dot_general | solution.py:14
  138.0 10.9 %convolution_convert_fusion.3 = bf16[640,2560]{1,0:T(8,128)(2,1)} fusion(bf16[2048,2560]{1,0:T(8,128)(2,1)} %get-tuple-element.36, bf16[2048,640]{0,1:T(8,128)(2,1)S(1)} %copy-done.4, f32[2048]{0:T(1024)S(1)} %add_rsqrt_fusion), kind=kOutput, calls=%fused_computation.39 | convolution fusion | flops 6716456960 | bytes 16392192 | tf_op jit(solution)/shard_map/dot_general | solution.py:14
  149.0 9.7 %fusion.51 = bf16[2048,640]{0,1:T(8,128)(2,1)S(1)} fusion(bf16[2048,2560]{1,0:T(8,128)(2,1)} %get-tuple-element.37, bf16[2,640,2560]{2,1,0:T(8,128)(2,1)S(1)} %bitcast.91), kind=kOutput, calls=%fused_computation.62 | convolution fusion | flops 6712197120 | bytes 16384000 | tf_op jit(solution)/shard_map/dot_general | solution.py:14
  158.7 11.1 %fusion.19 = (f32[2048]{0:T(1024)S(1)}, bf16[2048,640]{0,1:T(8,128)(2,1)}) fusion(bf16[2048,640]{0,1:T(8,128)(2,1)S(1)} %copy-done.4, bf16[2048,640]{0,1:T(8,128)(2,1)S(1)} %fusion.51, bf16[2048,2560]{1,0:T(8,128)(2,1)} %get-tuple-element.36, bf16[2,640,2560]{2,1,0:T(8,128)(2,1)S(1)} %bitcast.88), kind=kOutput, calls=%fused_computation.34 | convolution fusion | flops 6718748672 | bytes 21635072 | tf_op jit(solution)/shard_map/dot_general | solution.py:14
  169.8 3.0 copy.21
  172.8 0.0 slice-start.6
  172.8 4.5 fusion.64
  177.3 0.0 slice-start.7
  177.3 12.4 %convolution_convert_fusion.2 = bf16[2560,640]{1,0:T(8,128)(2,1)} fusion(bf16[2048,2560]{1,0:T(8,128)(2,1)} %get-tuple-element.38, bf16[2048,640]{0,1:T(8,128)(2,1)S(1)} %fusion.64), kind=kOutput, calls=%fused_computation.38 | convolution fusion | flops 6712524800 | bytes 16384000 | tf_op jit(solution)/shard_map/dot_general | solution.py:14
  189.7 11.4 %convolution_convert_fusion = bf16[2048,2560]{1,0:T(8,128)(2,1)} fusion(bf16[2048,640]{0,1:T(8,128)(2,1)S(1)} %fusion.64, bf16[2,2560,640]{2,1,0:T(8,128)(2,1)S(1)} %bitcast.94), kind=kOutput, calls=%fused_computation.16 | convolution fusion | flops 6716129280 | bytes 16384000 | tf_op jit(solution)/shard_map/dot_general | solution.py:14
  201.1 21.3 %fusion.24 = bf16[640,2560]{1,0:T(8,128)(2,1)} fusion(f32[2048,2560]{1,0:T(8,128)} %get-tuple-element.39, bf16[2048,2560]{1,0:T(8,128)(2,1)} %convolution_convert_fusion, f32[2048,2560]{1,0:T(8,128)} %fusion.43, bf16[1,2048,640]{1,2,0:T(8,128)(2,1)S(1)} %copy-done.1, f32[2048]{0:T(1024)S(1)} %copy-done.15), kind=kOutput, calls=%fused_computation.41 | convolution fusion | flops 6774128640 | bytes 58335232 | tf_op jit(solution)/shard_map/dot_general | solution.py:14
  222.4 15.6 %fusion.21 = bf16[640,2560]{1,0:T(8,128)(2,1)} fusion(bf16[2048,2560]{1,0:T(8,128)(2,1)} %convolution_convert_fusion, f32[2048,2560]{1,0:T(8,128)} %fusion.43, bf16[1,2048,640]{1,2,0:T(8,128)(2,1)S(1)} %copy-done.1, f32[2048]{0:T(1024)S(1)} %copy-done.15), kind=kOutput, calls=%fused_computation.37 | convolution fusion | flops 6753157120 | bytes 37363712 | tf_op jit(solution)/shard_map/dot_general | solution.py:14
  238.0 0.1 copy.22
  238.1 1.0 pad_maximum_fusion.refs_9_
  239.1 0.1 copy.24
  239.1 1.0 pad_maximum_fusion.1.refs_10_
  240.2 0.1 copy.26
  240.2 1.0 pad_maximum_fusion.2.refs_11_
  241.3 0.1 copy.28
  241.3 0.9 pad_maximum_fusion.3.refs_12_
  242.3 242.0 %reduce_step_gather.1 = (bf16[2,4,4,40,2560]{4,3,2,1,0:T(8,128)(2,1)}, bf16[2,4,4,40,2560]{4,3,2,1,0:T(8,128)(2,1)}, bf16[2,4,4,2,80,640]{5,4,3,2,1,0:T(8,128)(2...) custom-call(bf16[4,4,2,80,640]{4,3,2,1,0:T(8,128)(2,1)} %bitcast.102, ...), custom_call_target="tpu_custom_call" | custom-call | tf_op jit(solution)/shard_map/reduce_step_gather/pallas_call | solution.py:429
  484.4 1.7 slice_select_fusion.2
  486.1 1.1 copy.30
  487.2 1.1 copy.31
  488.2 1.7 slice_select_fusion
  490.0 1.1 copy.32
  491.1 1.1 copy.33
  492.1 3.3 copy.39
  495.5 0.1 slice-done.11
  495.5 3.3 copy.40
  498.9 0.7 slice-done.8
  499.6 1.0 slice-done.9
  500.5 2.8 copy.41
  503.3 0.8 copy.42
  504.1 0.8 copy.43
  (56 shorter events, 0.1 us)
Async XLA Ops:
  3.6 38.1 %copy-start = (bf16[1,2048,640]{1,2,0:T(8,128)(2,1)}, bf16[1,2048,640]{1,2,0:T(8,128)(2,1)S(1)}, u32[]{:S(2)}) copy-start(bf16[1,2048,640]{1,2,0:T(8,128)(2,1)S(1)} %copy.20) | copy-start | bytes 7864324
  3.7 16.7 %slice-start = ((s8[6553600]{0:T(1024)(128)(4,1)}), s8[4194304]{0:T(1024)(128)(4,1)S(1)}, s32[]{:S(2)}) async-start(s8[6553600]{0:T(1024)(128)(4,1)} %bitcast.85), calls=%async_computation | async-start | bytes 8388608
  4.2 16.1 %copy-start.14 = (f32[2048]{0:T(1024)}, f32[2048]{0:T(1024)S(1)}, u32[]{:S(2)}) copy-start(f32[2048]{0:T(1024)S(1)} %add_rsqrt_fusion.1) | copy-start | bytes 24580
  4.2 16.1 %slice-start.1 = ((s8[6553600]{0:T(1024)(128)(4,1)}), s8[2359296]{0:T(1024)(128)(4,1)S(1)}, s32[]{:S(2)}) async-start(s8[6553600]{0:T(1024)(128)(4,1)} %bitcast.85), calls=%async_computation.1 | async-start | bytes 4718592
  52.7 11.8 %copy-start.3 = (bf16[2048,640]{0,1:T(8,128)(2,1)}, bf16[2048,640]{0,1:T(8,128)(2,1)S(1)}, u32[]{:S(2)}) copy-start(bf16[2048,640]{0,1:T(8,128)(2,1)S(1)} %get-tuple-element.41) | copy-start | bytes 7864324
  52.8 11.7 %copy-start.12 = (f32[2048]{0:T(1024)}, f32[2048]{0:T(1024)S(1)}, u32[]{:S(2)}) copy-start(f32[2048]{0:T(1024)S(1)} %get-tuple-element.40) | copy-start | bytes 24580
  64.5 13.6 %copy-start.5 = (bf16[1,2048,640]{2,1,0:T(8,128)(2,1)S(1)}, bf16[1,2048,640]{2,1,0:T(8,128)(2,1)}, u32[]{:S(2)}) copy-start(bf16[1,2048,640]{2,1,0:T(8,128)(2,1)} %param.12) | copy-start | bytes 7864324
  97.1 30.0 %copy-start.4 = (bf16[2048,640]{0,1:T(8,128)(2,1)S(1)}, bf16[2048,640]{0,1:T(8,128)(2,1)}, u32[]{:S(2)}) copy-start(bf16[2048,640]{0,1:T(8,128)(2,1)} %copy-done.3) | copy-start | bytes 7864324
  127.1 21.9 %slice-start.4 = ((s8[6553600]{0:T(1024)(128)(4,1)}), s8[4194304]{0:T(1024)(128)(4,1)S(1)}, s32[]{:S(2)}) async-start(s8[6553600]{0:T(1024)(128)(4,1)} %bitcast.90), calls=%async_computation.4 | async-start | bytes 8388608
  127.1 31.6 %slice-start.2 = ((s8[6553600]{0:T(1024)(128)(4,1)}), s8[4194304]{0:T(1024)(128)(4,1)S(1)}, s32[]{:S(2)}) async-start(s8[6553600]{0:T(1024)(128)(4,1)} %bitcast.87), calls=%async_computation.2 | async-start | bytes 8388608
  138.0 10.9 %slice-start.5 = ((s8[6553600]{0:T(1024)(128)(4,1)}), s8[2359296]{0:T(1024)(128)(4,1)S(1)}, s32[]{:S(2)}) async-start(s8[6553600]{0:T(1024)(128)(4,1)} %bitcast.90), calls=%async_computation.5 | async-start | bytes 4718592
  138.0 20.6 %slice-start.3 = ((s8[6553600]{0:T(1024)(128)(4,1)}), s8[2359296]{0:T(1024)(128)(4,1)S(1)}, s32[]{:S(2)}) async-start(s8[6553600]{0:T(1024)(128)(4,1)} %bitcast.87), calls=%async_computation.3 | async-start | bytes 4718592
  158.7 14.1 %copy-start.13 = (f32[2048]{0:T(1024)S(1)}, f32[2048]{0:T(1024)}, u32[]{:S(2)}) copy-start(f32[2048]{0:T(1024)} %copy-done.12) | copy-start | bytes 24580
  172.8 16.9 %slice-start.6 = ((s8[6553600]{0:T(1024)(128)(4,1)}), s8[4194304]{0:T(1024)(128)(4,1)S(1)}, s32[]{:S(2)}) async-start(s8[6553600]{0:T(1024)(128)(4,1)} %bitcast.93), calls=%async_computation.6 | async-start | bytes 8388608
  177.3 12.4 %slice-start.7 = ((s8[6553600]{0:T(1024)(128)(4,1)}), s8[2359296]{0:T(1024)(128)(4,1)S(1)}, s32[]{:S(2)}) async-start(s8[6553600]{0:T(1024)(128)(4,1)} %bitcast.93), calls=%async_computation.7 | async-start | bytes 4718592
  189.7 11.4 %copy-start.1 = (bf16[1,2048,640]{1,2,0:T(8,128)(2,1)S(1)}, bf16[1,2048,640]{1,2,0:T(8,128)(2,1)}, u32[]{:S(2)}) copy-start(bf16[1,2048,640]{1,2,0:T(8,128)(2,1)} %copy-done) | copy-start | bytes 7864324
  189.7 11.4 %copy-start.15 = (f32[2048]{0:T(1024)S(1)}, f32[2048]{0:T(1024)}, u32[]{:S(2)}) copy-start(f32[2048]{0:T(1024)} %copy-done.14) | copy-start | bytes 24580
  222.4 15.6 %copy-start.6 = (f32[2,20,2560]{2,0,1:T(2,128)S(1)}, f32[2,20,2560]{2,0,1:T(2,128)}, u32[]{:S(2)}) copy-start(f32[2,20,2560]{2,0,1:T(2,128)} %param.16) | copy-start | bytes 1228804
  222.4 16.7 %copy-start.7 = (f32[2,20,2560]{2,0,1:T(2,128)S(1)}, f32[2,20,2560]{2,0,1:T(2,128)}, u32[]{:S(2)}) copy-start(f32[2,20,2560]{2,0,1:T(2,128)} %param.17) | copy-start | bytes 1228804
  222.4 17.8 %copy-start.8 = (f32[2,20,2560]{2,0,1:T(2,128)S(1)}, f32[2,20,2560]{2,0,1:T(2,128)}, u32[]{:S(2)}) copy-start(f32[2,20,2560]{2,0,1:T(2,128)} %param.19) | copy-start | bytes 1228804
  238.0 3.3 copy-start.9
  484.4 7.8 %copy-start.2 = (bf16[2,4,4,40,2560]{4,3,2,1,0:T(8,128)(2,1)S(1)}, bf16[2,4,4,40,2560]{4,3,2,1,0:T(8,128)(2,1)}, u32[]{:S(2)}) copy-start(bf16[2,4,4,40,2560]{4,3,2,1,0:T(8,128)(2,1)} %get-tuple-element.18) | copy-start | bytes 19660804
  488.2 7.2 %slice-start.10 = ((s8[6553600]{0:T(1024)(128)(4,1)}), s8[4194304]{0:T(1024)(128)(4,1)S(1)}, s32[]{:S(2)}) async-start(s8[6553600]{0:T(1024)(128)(4,1)} %bitcast.98), calls=%async_computation.10 | async-start | bytes 8388608
  492.1 3.4 slice-start.11
  492.1 7.4 %slice-start.8 = ((s8[6553600]{0:T(1024)(128)(4,1)}), s8[4194304]{0:T(1024)(128)(4,1)S(1)}, s32[]{:S(2)}) async-start(s8[6553600]{0:T(1024)(128)(4,1)} %bitcast.95), calls=%async_computation.8 | async-start | bytes 8388608
  495.5 5.0 slice-start.9
  500.5 2.8 copy-start.11
  500.5 3.5 copy-start.10

commit v3 on v2

--- a/solution.py
+++ b/solution.py
@@ -14,56 +14,96 @@
     return lax.dot_general(a, b, (((ca,), (cb,)), ((), ())), preferred_element_type=F32)
 
 
-def norm_scale(h):
-    wide = h.astype(F32)
-    return wide, lax.rsqrt(jnp.mean(wide**2, -1, keepdims=True) + 1e-6)
-
-
-def hidden(a, wg, wu):
-    gate, up = dot(a, wg, 1, 0), dot(a, wu, 1, 0)
-    return gate, up, (jax.nn.silu(gate) * up).astype(BF16)
-
-
-def hidden_back(ds, gate, up):
-    ds = ds.astype(F32)
-    sig = jax.nn.sigmoid(gate)
-    d_up = (ds * (gate * sig)).astype(BF16)
-    d_gate = (ds * up * (sig * (1 + gate * (1 - sig)))).astype(BF16)
-    return d_gate, d_up
-
-
-def gradients(x, dy, wg, wu, wd):
-    wide0, r0 = norm_scale(x)
-    a1 = (wide0 * r0).astype(BF16)
-    gate1, up1, s1 = hidden(a1, wg[0], wu[0])
-    h1 = x + dot(s1, wd[0], 1, 0).astype(BF16)
-    wide1, r1 = norm_scale(h1)
-    a2 = (wide1 * r1).astype(BF16)
-    gate2, up2, s2 = hidden(a2, wg[1], wu[1])
-
-    ds2 = dot(dy, wd[1], 1, 1).astype(BF16)
-    d_gate2, d_up2 = hidden_back(ds2, gate2, up2)
-    da2 = (dot(d_gate2, wg[1], 1, 1).astype(BF16) + dot(d_up2, wu[1], 1, 1).astype(BF16)).astype(F32)
-    back = da2 * r1 - wide1 * (r1**3 * jnp.mean(da2 * wide1, -1, keepdims=True))
-    dh1 = dy + back.astype(BF16)
-    ds1 = dot(dh1, wd[0], 1, 1).astype(BF16)
-    d_gate1, d_up1 = hidden_back(ds1, gate1, up1)
-
-    terms = ((a1, d_gate1), (a1, d_up1), (s1, dh1)), ((a2, d_gate2), (a2, d_up2), (s2, dy))
-    return [[dot(a, b, 0, 0).astype(BF16) for a, b in layer] for layer in terms]
+def states_kernel(x_ref, dy_ref, wg_hbm, wu_hbm, wd_hbm, a1t, a2t, dh1t, dyt, s1, s2, dg1, du1, dg2, du2, wg, wu, wd, silu1, slope1, sems):
+    width = min(512, wg.shape[2])
+    cuts = [slice(i, i + width) for i in range(0, wg.shape[2], width)]
+    first = pl.program_id(0) == 0
+    order = [(wg_hbm, wg, 0), (wu_hbm, wu, 0), (wd_hbm, wd, 0), (wg_hbm, wg, 1), (wu_hbm, wu, 1), (wd_hbm, wd, 1)]
+    copies = [pltpu.make_async_copy(src.at[layer], dst.at[layer], sems.at[i]) for i, (src, dst, layer) in enumerate(order)]
+
+    @pl.when(first)
+    def _():
+        for copy in copies:
+            copy.start()
+
+    def need(*which):
+        @pl.when(first)
+        def _():
+            for i in which:
+                copies[i].wait()
+
+    def normed(h):
+        wide = h.astype(F32)
+        r = lax.rsqrt(jnp.mean(wide * wide, -1, keepdims=True) + 1e-6)
+        return wide, r, (wide * r).astype(BF16)
+
+    def gated(a, layer, cut):
+        gate, up = dot(a, wg[layer, :, cut], 1, 0), dot(a, wu[layer, :, cut], 1, 0)
+        sig = 0.5 * jnp.tanh(0.5 * gate) + 0.5
+        silu = gate * sig
+        return silu, up * (sig + silu * (1 - sig)), (silu * up).astype(BF16)
+
+    def hidden_back(d, layer, cut, silu, slope):
+        ds = dot(d, wd[layer, cut, :], 1, 1).astype(BF16).astype(F32)
+        return (ds * slope).astype(BF16), (ds * silu).astype(BF16)
+
+    h0, dy = x_ref[...], dy_ref[...]
+    _, _, a1 = normed(h0)
+    need(0, 1)
+    for cut in cuts:
+        silu1[:, cut], slope1[:, cut], s1[:, cut] = gated(a1, 0, cut)
+    a1t[...] = a1.T
+    dyt[...] = dy.T
+    need(2)
+    h1 = (h0.astype(F32) + dot(s1[...], wd[0], 1, 0).astype(BF16).astype(F32)).astype(BF16)
+    wide1, r1, a2 = normed(h1)
+    need(3, 4, 5)
+    for cut in cuts:
+        silu, slope, s2[:, cut] = gated(a2, 1, cut)
+        dg2[:, cut], du2[:, cut] = hidden_back(dy, 1, cut, silu, slope)
+    a2t[...] = a2.T
+    by_gate, by_up = (dot(d[...], w[1], 1, 1).astype(BF16).astype(F32) for d, w in ((dg2, wg), (du2, wu)))
+    da2 = (by_gate + by_up).astype(BF16).astype(F32)
+    back = da2 * r1 - wide1 * (r1 * r1 * r1 * jnp.mean(da2 * wide1, -1, keepdims=True))
+    dh1 = (dy.astype(F32) + back.astype(BF16).astype(F32)).astype(BF16)
+    for cut in cuts:
+        dg1[:, cut], du1[:, cut] = hidden_back(dh1, 0, cut, silu1[:, cut], slope1[:, cut])
+    dh1t[...] = dh1.T
+
+
+def states(x, dy, wg, wu, wd):
+    (tokens, d), ff = x.shape, wg.shape[2]
+    block = min(256, tokens)
+    rows = pl.BlockSpec((block, d), lambda i: (i, 0))
+    flipped = pl.BlockSpec((d, block), lambda i: (0, i))
+    hidden = pl.BlockSpec((block, ff), lambda i: (i, 0))
+    return pl.pallas_call(
+        states_kernel,
+        grid=(tokens // block,),
+        out_shape=[jax.ShapeDtypeStruct((d, tokens), BF16)] * 4 + [jax.ShapeDtypeStruct((tokens, ff), BF16)] * 6,
+        in_specs=[rows, rows] + [pl.BlockSpec(memory_space=pl.ANY)] * 3,
+        out_specs=[flipped] * 4 + [hidden] * 6,
+        scratch_shapes=[pltpu.VMEM(w.shape, BF16) for w in (wg, wu, wd)]
+        + [pltpu.VMEM((block, ff), F32)] * 2
+        + [pltpu.SemaphoreType.DMA((6,))],
+        compiler_params=pltpu.CompilerParams(vmem_limit_bytes=60 * 2**20),
+        name="states",
+    )(x, dy, wg, wu, wd)
 
 
 MESH = pl.DeviceIdType.MESH
 MATRICES = (("d", 0, 1, 2), ("w", 0, 1, 0), ("w", 1, 1, 1), ("d", 1, 0, 2), ("w", 2, 0, 0), ("w", 3, 0, 1))
 SIX = range(6)
+LEFT = (0, 1, 1, 2, 3, 3)
 
 
 def step_kernel(count, *refs):
-    terms, weights, moments, out_w, out_m = refs[0:6], refs[6:9], refs[9:15], refs[15:18], refs[18:24]
-    own_w, own_d, two_w, two_d, r1_w, r1_d, r2_w, r2_d, zl_w, zl_d, zr_w, zr_d = refs[24:36]
-    tmp_w, tmp_d, g_w, g_d, state_w, state_d, old_w, old_d, new_w, got_w, norm = refs[36:47]
+    lefts, rights, weights, moments, out_w, out_m = refs[0:4], refs[4:10], refs[10:13], refs[13:19], refs[19:22], refs[22:28]
+    own_w, own_d, two_w, two_d, r1_w, r1_d, r2_w, r2_d, zl_w, zl_d, zr_w, zr_d = refs[28:40]
+    tmp_w, tmp_d, g_w, g_d, state_w, state_d, old_w, old_d, new_w, got_w, norm = refs[40:51]
     (loc_sem, aux_sem, two_s, two_r, s1_s, s1_r, s2_s, s2_r, z_s, zl_r, zr_r, g_s, g_r, n_s, n_r, nz_r, w_s, w_r, ag_r, agz_s, ag1_s, ag2_s,
-     ag3_s, agt_s, agt_r, out_s, out2_s) = refs[47:74]
+     ag3_s, agt_s, agt_r, out_s, out2_s) = refs[51:78]
+    left_v, right_v, stage_w, stage_d, left_sem, right_sem = refs[78:84]
     own, two = {"w": own_w, "d": own_d}, {"w": two_w, "d": two_d}
     r1, r2 = {"w": r1_w, "d": r1_d}, {"w": r2_w, "d": r2_d}
     zl, zr, tmp = {"w": zl_w, "d": zl_d}, {"w": zr_w, "d": zr_d}, {"w": tmp_w, "d": tmp_d}
@@ -91,20 +131,68 @@
         pl.semaphore_signal(barrier, inc=1, device_id=other, device_id_type=MESH)
     pl.semaphore_wait(barrier, 6)
 
-    def half_of(j, c):
-        return terms[j].at[:, :, :, columns(c)] if MATRICES[j][0] == "w" else terms[j].at[:, :, c]
-
     def to_partner(j):
         kind, t, _, _ = MATRICES[j]
-        return remote(half_of(j, 1 - core), two[kind].at[t], two_s.at[j], two_r.at[j], partner)
-
-    def bring(j):
-        kind, t, _, _ = MATRICES[j]
-        return pltpu.make_async_copy(half_of(j, core), own[kind].at[t], loc_sem.at[j])
-
-    for j in SIX:
-        to_partner(j).start()
-        bring(j).start()
+        return remote(stage_w.at[t % 2] if kind == "w" else stage_d, two[kind].at[t], two_s.at[j], two_r.at[j], partner)
+
+    def left_copy(i):
+        return pltpu.make_async_copy(lefts[i], left_v.at[i % 2], left_sem.at[i])
+
+    def right_copy(n):
+        j, part = n // 2, n % 2
+        if MATRICES[j][0] == "w":
+            part = core if part else 1 - core
+        size = right_v.shape[2]
+        return pltpu.make_async_copy(rights[j].at[:, pl.ds(pl.multiple_of(part * size, 128), size)], right_v.at[n % 2], right_sem.at[n])
+
+    def make(j):
+        kind, t, _, _ = MATRICES[j]
+        factor_l = left_v.at[LEFT[j] % 2]
+        if j == 0 or LEFT[j] != LEFT[j - 1]:
+            left_copy(LEFT[j]).wait()
+        if kind == "w" and t >= 2:
+            to_partner(j - 3).wait_send()
+        if kind == "d" and t:
+            to_partner(j - 3).wait_send()
+        for part in range(2):
+            n = 2 * j + part
+            right_copy(n).wait()
+            factor_r = right_v.at[n % 2]
+            if kind == "w":
+                width = min(256, half)
+
+                @pl.loop(0, half // width)
+                def _(q):
+                    cut = pl.ds(pl.multiple_of(q * width, width), width)
+                    made = dot(factor_l[...], factor_r[:, cut], 1, 0).astype(BF16)
+                    made = made.reshape(4, 4, own_w.shape[3], width)
+                    if part:
+                        own_w[t, :, :, :, cut] = made
+                    else:
+                        stage_w[t % 2, :, :, :, cut] = made
+
+                if part == 0:
+                    to_partner(j).start()
+            else:
+                width = factor_r.shape[1] // 2
+
+                @pl.loop(0, 2)
+                def _(q):
+                    made = dot(factor_l[...], factor_r[:, pl.ds(pl.multiple_of(q * width, width), width)], 1, 0).T
+                    made = made.reshape(4, 2, *own_d.shape[3:])
+                    own_d[t, part * 2 + q] = jnp.where(core == 0, made[:, 0], made[:, 1]).astype(BF16)
+                    stage_d[part * 2 + q] = jnp.where(core == 0, made[:, 1], made[:, 0]).astype(BF16)
+
+                if part:
+                    to_partner(j).start()
+            if n + 2 < 12:
+                right_copy(n + 2).start()
+        if j in (0, 2):
+            left_copy(LEFT[j] + 2).start()
+
+    for i in range(2):
+        left_copy(i).start()
+        right_copy(i).start()
     chip = (x * 2 + y, z)
     aux = [pltpu.make_async_copy(moments[i], (state_w, state_w, state_w, state_w, state_d, state_d)[i].at[(0, 1, 2, 3, 0, 1)[i]], aux_sem.at[i]) for i in SIX]
     aux += [pltpu.make_async_copy(weights[i].at[:, chip[0], chip[1]], old_w.at[i], aux_sem.at[6 + i]) for i in range(2)]
@@ -136,10 +224,9 @@
         land, sems = (zl, zl_r) if rightward else (zr, zr_r)
         return remote(own[kind].at[t, chip[0], to], land[kind].at[t, to], z_s.at[j, to], sems.at[j, to], right if rightward else left)
 
-    for j in SIX:
+    def leave_first(j):
         kind, t, _, _ = MATRICES[j]
         to_partner(j).wait_recv()
-        bring(j).wait()
         for i in range(2):
             group, copy = first(j, i)
 
@@ -148,7 +235,8 @@
                 add_into(own[kind].at[t, group, b], own[kind].at[t, group, b], two[kind].at[t, group, b])
 
             copy.start()
-    for j in SIX:
+
+    def leave_second(j):
         kind, t, _, _ = MATRICES[j]
         for i in range(2):
             first(j, i)[1].wait_recv()
@@ -159,6 +247,14 @@
             add_into(own[kind].at[t, group, b], own[kind].at[t, group, b], two[kind].at[t, group, b], r1[kind].at[t, i, b])
 
         copy.start()
+
+    for j in SIX:
+        make(j)
+        leave_first(j)
+        if j >= 3:
+            leave_second(j - 3)
+    for j in (3, 4, 5):
+        leave_second(j)
 
     def partial(j, to):
         kind, t, _, _ = MATRICES[j]
@@ -219,7 +315,8 @@
                 squares = part * part if squares is None else squares + part * part
 
     for j in SIX:
-        to_partner(j).wait_send()
+        if j >= 3:
+            to_partner(j).wait_send()
         for i in range(2):
             first(j, i)[1].wait_send()
         second(j)[2].wait_send()
@@ -407,10 +504,9 @@
             put(j, group, 1 - core, two, out2_s.at[j, i]).wait()
 
 
-def reduce_step_gather(terms, weights, moments):
-    wide = next(t for t, m in zip(terms, MATRICES) if m[0] == "w").shape
-    down = terms[0].shape
-    rw, cw, rd, cd = wide[2], wide[3] // 2, down[3], down[4]
+def reduce_step_gather(lefts, rights, weights, moments):
+    (d_model, tokens), ff = lefts[0].shape, rights[0].shape[1]
+    rw, cw, rd, cd = d_model // 16, ff // 2, ff // 32, d_model
     count = 4 * 16 * rw * 2 * cw + 2 * 32 * rd * cd
     vm, dma = pltpu.VMEM, pltpu.SemaphoreType.DMA
     w, d = (rw, cw), (rd, cd)
@@ -424,20 +520,21 @@
         dma((6,)), dma((9,)), dma((6,)), dma((6,)), dma((6, 2)), dma((6, 2)), dma((6,)), dma((6,)), dma((6, 4)), dma((6, 4)), dma((6, 4)),
         dma((4,)), dma((4,)), dma((6,)), dma((3,)), dma((4,)), dma((4,)), dma((4,)),
         dma((6, 4, 4)), dma((6, 4, 2)), dma((6, 4)), dma((6, 4)), dma((6, 4)), dma((6, 4)), dma((6, 4)), dma((6, 4)), dma((6, 4)),
+        vm((2, d_model, tokens), BF16), vm((2, tokens, ff // 2), BF16), vm((2, 4, 4, *w), BF16), vm((4, 4, *d), BF16), dma((4,)), dma((12,)),
     ]
     outs = [jax.ShapeDtypeStruct(a.shape, a.dtype) for a in (*weights, *moments)]
     return pl.pallas_call(
         functools.partial(step_kernel, count),
         out_shape=outs,
-        in_specs=[pl.BlockSpec(memory_space=pl.ANY)] * 15,
+        in_specs=[pl.BlockSpec(memory_space=pl.ANY)] * 19,
         out_specs=[pl.BlockSpec(memory_space=pl.ANY)] * 9,
         scratch_shapes=scratch,
-        compiler_params=pltpu.CompilerParams(collective_id=0, has_side_effects=True, vmem_limit_bytes=60 * 2**20),
+        compiler_params=pltpu.CompilerParams(collective_id=0, has_side_effects=True, vmem_limit_bytes=67043328),
         name="reduce_step_gather",
-    )(*terms, *weights, *moments)
-
-
-def all_steps(me, terms, w, m, v):
+    )(*lefts, *rights, *weights, *moments)
+
+
+def all_steps(me, lefts, rights, w, m, v):
     core = me % 2
 
     def blocks(t):
@@ -446,10 +543,9 @@
     def down_blocks(t):
         return t.reshape(*t.shape[:-2], 4, 4, 2, t.shape[-2] // 32, t.shape[-1])
 
-    ordered = [(blocks if kind == "w" else down_blocks)(terms[layer][arg]) for kind, _, layer, arg in MATRICES]
     twice = [jnp.concatenate([t, t], axis=1) for t in (m[0], m[1], v[0], v[1])]
     weights = [blocks(w[0]), blocks(w[1]), down_blocks(w[2])]
-    out = reduce_step_gather(ordered, weights, [*twice, m[2], v[2]])
+    out = reduce_step_gather(lefts, rights, weights, [*twice, m[2], v[2]])
     new = [a.reshape(b.shape) for a, b in zip(out[:3], w)]
     rows = m[0].shape[1]
     mine = [jnp.where(core == 0, t[:, :rows], t[:, rows:]) for t in out[3:7]]
@@ -459,7 +555,8 @@
 def solution(mesh):
     def body(x, dy, *arrays):
         w, m, v = (arrays[i : i + 3] for i in (0, 3, 6))
-        return all_steps(lax.axis_index("dp"), gradients(x[0], dy[0], *w), w, m, v)
+        a1t, a2t, dh1t, dyt, s1, s2, dg1, du1, dg2, du2 = states(x[0], dy[0], *w)
+        return all_steps(lax.axis_index("dp"), (dyt, a2t, dh1t, a1t), (s2, dg2, du2, s1, dg1, du1), w, m, v)
 
     moments = P(None, "dp", None)
     return jax.shard_map(

time: 513 us -> 388 us (0.76); the launches traced: 505 us -> 388 us
  matrix products: 226 us -> 0 us
  Pallas kernels: 242 us -> 363 us
  local copies, waits for them, and re-layouts: 23.3 us -> 17.3 us
  other arithmetic: 12.5 us -> 7.36 us
    dot_general x15 -> x0, matrix products: 226 us -> none  [dot(): lax.dot_general(a, b, (((ca,), (cb,)), ((), ())), preferred_element_type=...]
    pallas_call x0 -> x1, Pallas kernels: none -> 93.9 us  [states(): pl.pallas_call(states_kernel, grid=(tokens // block,), out_shape=[jax.Sha...]
    pallas_call x1, Pallas kernels: 242 us -> 269 us  [reduce_step_gather(): pl.pallas_call(functools.partial(step_kernel, count), out_shape=outs, in_...]
    unnamed x71 -> x35, local copies, waits for them, and re-layouts: 23.3 us -> 17.3 us
where the time goes in v3:
time: 388 us
  Pallas kernels  363 us (94%)
  local copies, waits for them, and re-layouts  17.3 us (4%)
  other arithmetic  7.36 us (2%)
    pallas_call x1, Pallas kernels, reduce_step_gather(): pl.pallas_call(functools.partial(step_kernel, count), out_shape=outs, in_...  269 us
    pallas_call x1, Pallas kernels, states(): pl.pallas_call(states_kernel, grid=(tokens // block,), out_shape=[jax.Sha...  93.9 us
    unnamed x35, local copies, waits for them, and re-layouts  17.3 us

profile of v3, /device:TPU:0, one launch (start us, length us, event | category | flops | bytes accessed | tf_op | source)
XLA Modules:
  0.0 388.2 jit_solution(4519024214694215452)
XLA Ops:
  0.6 0.0 copy-start.1
  0.7 0.0 copy-start.2
  0.7 0.0 copy-start.3
  0.7 93.9 %states.1 = (bf16[640,2048]{1,0:T(8,128)(2,1)}, bf16[640,2048]{1,0:T(8,128)(2,1)}, bf16[640,2048]{1,0:T(8,128)(2,1)}, bf16[640,2048]{1,0:T(8,128)(2,1)}, bf16[20...) custom-call(bf16[2048,640]{1,0:T(8,128)(2,1)} %bitcast.18, ...), custom_call_target="tpu_custom_call" | custom-call | tf_op jit(solution)/shard_map/states/pallas_call | solution.py:80
  94.6 0.0 copy-start.4
  94.6 0.0 copy-done.1
  94.6 0.1 copy.20
  94.7 1.0 pad_maximum_fusion.refs_13_
  95.7 0.0 copy-done.2
  95.7 0.1 copy.22
  95.7 1.0 pad_maximum_fusion.1.refs_14_
  96.7 0.0 copy-done.3
  96.7 0.1 copy.24
  96.8 1.0 pad_maximum_fusion.2.refs_15_
  97.8 0.0 copy-done.4
  97.8 0.1 copy.26
  97.9 1.0 pad_maximum_fusion.3.refs_16_
  98.8 268.9 %reduce_step_gather.1 = (bf16[2,4,4,40,2560]{4,3,2,1,0:T(8,128)(2,1)}, bf16[2,4,4,40,2560]{4,3,2,1,0:T(8,128)(2,1)}, bf16[2,4,4,2,80,640]{5,4,3,2,1,0:T(8,128)(2...) custom-call(bf16[640,2048]{1,0:T(8,128)(2,1)} %get-tuple-element.28., ...), custom_call_target="tpu_custom_call" | custom-call | tf_op jit(solution)/shard_map/reduce_step_gather/pallas_call | solution.py:526
  367.8 0.0 copy-start
  367.8 1.7 slice_select_fusion
  369.5 1.1 copy.30
  370.6 1.1 copy.31
  371.6 0.0 slice-start.2
  371.7 1.7 slice_select_fusion.2
  373.4 1.1 copy.28
  374.5 1.1 copy.29
  375.5 0.0 copy-done
  375.5 0.0 slice-start.3
  375.5 0.0 slice-start
  375.5 3.3 copy.37
  378.9 0.0 slice-done.2
  378.9 0.1 slice-done.3
  378.9 0.0 slice-start.1
  378.9 3.3 copy.38
  382.3 0.7 slice-done
  383.0 1.0 slice-done.1
  383.9 0.0 copy-start.6
  383.9 0.0 copy-start.5
  383.9 2.8 copy.39
  386.7 0.0 copy-done.6
  386.7 0.8 copy.40
  387.5 0.0 copy-done.5
  387.5 0.8 copy.41
  (2 shorter events, 0.0 us)
Async XLA Ops:
  0.6 94.0 %copy-start.1 = (f32[2,20,2560]{2,0,1:T(2,128)S(1)}, f32[2,20,2560]{2,0,1:T(2,128)}, u32[]{:S(2)}) copy-start(f32[2,20,2560]{2,0,1:T(2,128)} %param.16) | copy-start | bytes 1228804
  0.7 95.0 %copy-start.2 = (f32[2,20,2560]{2,0,1:T(2,128)S(1)}, f32[2,20,2560]{2,0,1:T(2,128)}, u32[]{:S(2)}) copy-start(f32[2,20,2560]{2,0,1:T(2,128)} %param.17) | copy-start | bytes 1228804
  0.7 96.1 %copy-start.3 = (f32[2,20,2560]{2,0,1:T(2,128)S(1)}, f32[2,20,2560]{2,0,1:T(2,128)}, u32[]{:S(2)}) copy-start(f32[2,20,2560]{2,0,1:T(2,128)} %param.19) | copy-start | bytes 1228804
  94.6 3.2 copy-start.4
  367.8 7.8 %copy-start = (bf16[2,4,4,40,2560]{4,3,2,1,0:T(8,128)(2,1)S(1)}, bf16[2,4,4,40,2560]{4,3,2,1,0:T(8,128)(2,1)}, u32[]{:S(2)}) copy-start(bf16[2,4,4,40,2560]{4,3,2,1,0:T(8,128)(2,1)} %get-tuple-element.38) | copy-start | bytes 19660804
  371.6 7.2 %slice-start.2 = ((s8[6553600]{0:T(1024)(128)(4,1)}), s8[4194304]{0:T(1024)(128)(4,1)S(1)}, s32[]{:S(2)}) async-start(s8[6553600]{0:T(1024)(128)(4,1)} %bitcast.14), calls=%async_computation.2 | async-start | bytes 8388608
  375.5 3.4 slice-start.3
  375.5 7.4 %slice-start = ((s8[6553600]{0:T(1024)(128)(4,1)}), s8[4194304]{0:T(1024)(128)(4,1)S(1)}, s32[]{:S(2)}) async-start(s8[6553600]{0:T(1024)(128)(4,1)} %bitcast.11), calls=%async_computation | async-start | bytes 8388608
  378.9 5.0 %slice-start.1 = ((s8[6553600]{0:T(1024)(128)(4,1)}), s8[2359296]{0:T(1024)(128)(4,1)S(1)}, s32[]{:S(2)}) async-start(s8[6553600]{0:T(1024)(128)(4,1)} %bitcast.11), calls=%async_computation.1 | async-start | bytes 4718592
  383.9 2.8 copy-start.6
  383.9 3.5 copy-start.5
